TPU v7x, 32 devices: a whole 2x2x4 slice. The times are simulated.
32 devices in a mesh: pipe: 4 (over z), dp: 4 (over y, x), tensor: 2 (over core).
Axes of the slice: x: 2, y: 2, z: 4, core: 2. Of those that a mesh axis runs over, the one named last changes fastest.
Arguments:
- saved_inputs: bfloat16 [3, 2, 4, 512, 4096], P(None, None, 'pipe', 'dp', 'tensor'), may hold values from -6 to 6
- proj_in: bfloat16 [2, 4, 512, 4096], P(None, 'pipe', None, 'tensor'), may hold values from -0.09375 to 0.09375
- proj_out: bfloat16 [2, 4, 512, 4096], P(None, 'pipe', None, 'tensor'), may hold values from -0.25 to 0.25
- norm_gain: float32 [2, 4, 4096], P(None, 'pipe', 'tensor'), may hold values from 0.1 to 1.9
- arriving: bfloat16 [2, 4, 512, 4096], P(None, 'pipe', 'dp', 'tensor'), may hold values from -6 to 6
- logp_grad: bfloat16 [2, 512, 4096], P(None, 'dp', 'tensor'), may hold values from -6 to 6
- rewards: float32 [2, 4, 4], P(None, 'dp'), may hold values from -4 to 4
- seq_lengths: int32 [2, 4, 4], P(None, 'dp'), may hold values from 1 to 64, 128 in all within a row
- group_ids: int32 [2, 4, 4], P(None, 'dp'), may hold values from 0 to 3
Outputs:
- grad_in: float32 [2, 4, 512, 4096], P(None, 'pipe', 'dp', 'tensor')
- grad_out: float32 [2, 4, 512, 4096], P(None, 'pipe', 'dp', 'tensor')
- leaving: bfloat16 [2, 4, 512, 4096], P(None, 'pipe', 'dp', 'tensor')
Inputs may be any that keep to these rules, and one draw needn't show every extreme that they name: `seq_lengths`: the 4 lengths of one microbatch on one replica sum to 128. `group_ids`: groups take sequences from several replicas and microbatches.
All inputs are finite; a program needn't handle non-finite values.
Results may differ from a plain program's by a relative error of at most 0.023.
Values may be sent and summed in bfloat16 or wider, within the bound.
A program may use at most 128 MiB of HBM per device.

v0:
```python
import functools

import jax
import jax.numpy as jnp
from jax import lax
from jax.experimental import pallas as pl
from jax.experimental.pallas import tpu as pltpu
from jax.sharding import PartitionSpec as P

EPS = 1e-05
MESH = pl.DeviceIdType.MESH
F32 = jnp.float32
BF16 = jnp.bfloat16


def dot_nt(a, b):
    return lax.dot_general(a, b, (((1,), (1,)), ((), ())), preferred_element_type=F32)


def factors(n):
    low = 1
    for k in range(1, n + 1):
        if n % k == 0 and k * k <= n:
            low = k
    return low, n // low


def kernel(
    dims,
    x_hbm, wi_hbm, wo_hbm, gn_ref, ar_hbm, lp_hbm, rew_ref, len_ref, ids_ref,
    fi, fo, lv,
    xs, gd, ca, wi, wo, lp, ps, pr, presum, slope, hid_t, gs, gs_t, gsr0, gsr1, gdr0, gdr1, bs, br, ob,
    sqs, sqr, inv_t, stl, str_, gba, gbb, r1a, r1b, p2a, p2b, r2a, r2b, p2i0, p2i1, r2i0, r2i1,
    in_sem, sq_sem, st_sem, pre_sem, back_sem, pipe_s, pipe_r, gd_s, gd_r, gt_s, gt_r,
    r1_s, r1_r, r2_s, r2_r,
):
    steps, vs, tok, wid, rank, nt, npipe, ndp = dims
    na, nb = factors(ndp)
    rc = rank // ndp
    full = wid * nt
    tile = min(512, wid // 2)
    rtile = min(512, rank)
    half = wid // 2
    lanes = stl.shape[1]
    new_count, _, seq_count = rew_ref.shape
    unit_lane = new_count * ndp * seq_count // 8
    me_t = lax.axis_index("tensor")
    me_p = lax.axis_index("pipe")
    me_d = lax.axis_index("dp")
    me_h = me_d // nb
    me_l = me_d % nb
    prev_p = lax.rem(me_p + npipe - 1, npipe)
    next_p = lax.rem(me_p + 1, npipe)

    def load(src, dst, k):
        return pltpu.make_async_copy(src, dst, in_sem.at[k])

    loads = [
        load(ar_hbm.at[1], ca.at[1, 0], 0),
        load(wo_hbm.at[1], wo.at[1], 1),
        load(x_hbm.at[:, 1], xs.at[:, 1], 2),
        load(wi_hbm.at[1], wi.at[1], 3),
        load(x_hbm.at[:, 0], xs.at[:, 0], 4),
        load(ar_hbm.at[0], ca.at[0, 0], 5),
        load(wo_hbm.at[0], wo.at[0], 6),
        load(wi_hbm.at[0], wi.at[0], 7),
        load(lp_hbm, lp, 8),
    ]
    for item in loads:
        item.start()

    lane8 = lax.broadcasted_iota(jnp.int32, (8, lanes), 1)
    row8 = lax.broadcasted_iota(jnp.int32, (8, lanes), 0)
    stats_own = jnp.where((row8 == 2) & (lane8 == unit_lane), 1.0, 0.0)
    for n in range(new_count):
        for k in range(seq_count):
            value = jnp.where(row8 == 0, rew_ref[n, 0, k], jnp.where(row8 == 1, 1.0, 0.0))
            stats_own = stats_own + jnp.where(lane8 == ids_ref[n, 0, k], value, 0.0)
    stl[...] = stats_own

    barrier = pltpu.get_barrier_semaphore()
    for k in range(1, nt):
        pl.semaphore_signal(barrier, inc=1, device_id={"tensor": lax.rem(me_t + k, nt)}, device_id_type=MESH)
    for k in range(1, ndp):
        pl.semaphore_signal(barrier, inc=1, device_id={"dp": lax.rem(me_d + k, ndp)}, device_id_type=MESH)
    for other in (prev_p, next_p):
        pl.semaphore_signal(barrier, inc=1, device_id={"pipe": other}, device_id_type=MESH)
    pl.semaphore_wait(barrier, nt - 1 + ndp - 1 + 2)

    def to_tensor(src, dst_of, send_of, recv_of):
        return [
            pltpu.make_async_remote_copy(
                src_ref=src, dst_ref=dst_of(k - 1), send_sem=send_of(k - 1), recv_sem=recv_of(k - 1),
                device_id={"tensor": lax.rem(me_t + k, nt)}, device_id_type=MESH,
            )
            for k in range(1, nt)
        ]

    def to_dp(src_of, dst_of, send_of, recv_of, kind):
        out = []
        count = {"all": ndp, "h": na, "l": nb}[kind]
        for k in range(1, count):
            if kind == "all":
                who = lax.rem(me_d + k, ndp)
                part = who
            elif kind == "h":
                part = lax.rem(me_h + k, na)
                who = part * nb + me_l
            else:
                part = lax.rem(me_l + k, nb)
                who = me_h * nb + part
            out.append(
                pltpu.make_async_remote_copy(
                    src_ref=src_of(part), dst_ref=dst_of(k - 1), send_sem=send_of(k - 1), recv_sem=recv_of(k - 1),
                    device_id={"dp": who}, device_id_type=MESH,
                )
            )
        return out

    stat_copies = to_dp(lambda part: stl, lambda k: str_.at[k], lambda k: st_sem.at[0, k], lambda k: st_sem.at[1, k], "all")
    for item in stat_copies:
        item.start()

    lane = lax.broadcasted_iota(jnp.int32, (tok, 128), 1)

    def sq_copies(v):
        return to_tensor(
            sqs.at[v], lambda k: sqr.at[k, v], lambda k: sq_sem.at[0, v, k], lambda k: sq_sem.at[1, v, k]
        )

    def prep(v):
        def body(t, squares_all):
            row = xs[t, v].astype(F32)
            gd[v, pl.ds(pl.multiple_of(t * tok, tok), tok), :] = (row * gn_ref[v]).astype(BF16)
            squares = jnp.sum(row * row, axis=-1, keepdims=True)
            return jnp.where(lane == t, squares, squares_all)

        sqs[v] = lax.fori_loop(0, steps, body, jnp.zeros((tok, 128), F32))
        for item in sq_copies(v) + gd_copies(v):
            item.start()

    def finish_sq(v):
        for item in sq_copies(v):
            item.wait_recv()
        total = sqs[v]
        for k in range(nt - 1):
            total = total + sqr[k, v]
        inv_t[v] = 1.0 / jnp.sqrt(total * (1.0 / full) + EPS)

    gather_kind = ("h", "l")
    gdr = (gdr0, gdr1)
    gsr = (gsr0, gsr1)

    def gd_copies(v):
        return to_dp(
            lambda part: gd.at[v], lambda k: gdr[v].at[k],
            lambda k: gd_s.at[v, k], lambda k: gd_r.at[v, k], gather_kind[v],
        )

    def gs_copies(t, v):
        cols = pl.ds(t * tok, tok)
        base = v * steps + t
        source = (lambda part: gs_t.at[v, part, :, :, cols]) if v == 0 else (lambda part: gs_t.at[v, :, part, :, cols])
        return to_dp(
            source, lambda k: gsr[v].at[k, :, :, cols],
            lambda k: gt_s.at[base, k], lambda k: gt_r.at[base, k], gather_kind[v],
        )

    pre_copies = {}
    back_copies = {}

    def pre_part(v):
        def body(j, carry):
            cols = pl.ds(pl.multiple_of(j * rtile, rtile), rtile)
            ps[v, :, cols] = dot_nt(gd[v], wi[v, cols, :]).astype(BF16)
            return carry

        lax.fori_loop(0, rank // rtile, body, 0)
        pre_copies[v] = to_tensor(
            ps.at[v], lambda k: pr.at[k, v], lambda k: pre_sem.at[0, v, k], lambda k: pre_sem.at[1, v, k]
        )
        for item in pre_copies[v]:
            item.start()

    def back_part(t, v):
        def body(j, carry):
            cols = pl.ds(pl.multiple_of(j * rtile, rtile), rtile)
            bs[v, t, :, cols] = dot_nt(ca[v, t], wo[v, cols, :]).astype(BF16)
            return carry

        lax.fori_loop(0, rank // rtile, body, 0)
        back_copies[t, v] = to_tensor(
            bs.at[v, t], lambda k: br.at[k, v, t],
            lambda k: back_sem.at[0, v * steps + t, k], lambda k: back_sem.at[1, v * steps + t, k],
        )
        for item in back_copies[t, v]:
            item.start()

    def finish_pre(v, which_steps):
        for t in which_steps:
            rows = pl.ds(t * tok, tok)
            total = ps[v, rows, :].astype(F32)
            for k in range(nt - 1):
                total = total + pr[k, v, rows, :].astype(F32)
            pre = inv_t[v, :, t:t + 1] * total
            sigma = jax.nn.sigmoid(pre)
            presum[v, rows, :] = total
            hid_t[v, :, rows] = jnp.transpose(pre * sigma).astype(BF16)
            slope[v, rows, :] = sigma * (1.0 + pre * (1.0 - sigma))

    def finish_back(t, v):
        for item in back_copies[t, v]:
            item.wait_recv()
        rows = pl.ds(t * tok, tok)
        inv = inv_t[v, :, t:t + 1]
        total = bs[v, t].astype(F32)
        for k in range(nt - 1):
            total = total + br[k, v, t].astype(F32)
        grad_pre = total * slope[v, rows, :]
        scaled = inv * grad_pre
        gs[v, rows, :] = scaled.astype(BF16)
        gs_t[v, :, :, :, rows] = jnp.transpose(scaled).astype(BF16).reshape(na, nb, rc, tok)
        for item in gs_copies(t, v):
            item.start()
        if t == steps - 1:
            for item in copies_one(0, v) + copies_one(1, v):
                item.start()
        radial = jnp.sum(grad_pre * presum[v, rows, :], axis=-1, keepdims=True)
        coef = inv * inv * inv * radial * (1.0 / full)

        def body(j, carry):
            cols = pl.ds(pl.multiple_of(j * tile, tile), tile)
            lifted = jnp.dot(gs[v, rows, :], wi[v, :, cols], preferred_element_type=F32)
            out = (
                ca[v, t, :, cols].astype(F32)
                + gn_ref[v, :, cols] * lifted
                - xs[t, v, :, cols].astype(F32) * coef
            ).astype(BF16)
            if t < steps - 1:
                ob[t, v, :, cols] = out
            else:
                lv[v, :, cols] = out
            return carry

        lax.fori_loop(0, wid // tile, body, 0)

    half_tok = tok // 2

    def pipe_copies(t, v, slot):
        parts = [(0, half_tok), (half_tok, half_tok)] if slot == 0 else [(0, tok)]
        return [
            pltpu.make_async_remote_copy(
                src_ref=ob.at[t, v, pl.ds(start, size)], dst_ref=ca.at[slot, t + 1, pl.ds(start, size)],
                send_sem=pipe_s.at[t, v, k], recv_sem=pipe_r.at[t, slot, k],
                device_id={"pipe": prev_p}, device_id_type=MESH,
            )
            for k, (start, size) in enumerate(parts)
        ]

    def send_on(t, v, first, last):
        @pl.when(me_p > 0)
        def _():
            for item in pipe_copies(t, v, v)[first:last]:
                item.start()

        if v == 1:
            @pl.when(me_p == 0)
            def _():
                for item in pipe_copies(t, 1, 0):
                    item.start()

    def sent_on(t, v):
        @pl.when(me_p > 0)
        def _():
            for item in pipe_copies(t, v, v):
                item.wait_send()

        if v == 1:
            @pl.when(me_p == 0)
            def _():
                for item in pipe_copies(t, 1, 0):
                    item.wait_send()

    def take(t, v):
        if v == 0:
            for item in pipe_copies(t - 1, v, v):
                item.wait_recv()
        else:
            @pl.when(me_p < npipe - 1)
            def _():
                for item in pipe_copies(t - 1, v, v):
                    item.wait_recv()

            @pl.when(me_p == npipe - 1)
            def _():
                stats = stl[...]
                for k in range(ndp - 1):
                    stats = stats + str_[k]
                means = stats[0:1] / jnp.maximum(stats[1:2], 1.0) + stats[2:3] * (1.0 / ndp)
                tok_row = lax.broadcasted_iota(jnp.int32, (tok, lanes), 0)
                tok_lane = lax.broadcasted_iota(jnp.int32, (tok, lanes), 1)
                hot = jnp.zeros((tok, lanes), F32)
                begin = 0
                for k in range(seq_count):
                    finish = begin + len_ref[t - 1, 0, k]
                    inside = (tok_row >= begin) & (tok_row < finish)
                    value = jnp.where(tok_lane == ids_ref[t - 1, 0, k], 1.0, 0.0)
                    value = value - jnp.where(tok_lane == unit_lane, rew_ref[t - 1, 0, k], 0.0)
                    hot = hot + jnp.where(inside, value, 0.0)
                    begin = finish
                weight = jnp.sum(hot * means, axis=-1, keepdims=True)
                ca[1, t] = (weight * lp[t - 1].astype(F32)).astype(BF16)

    def grad_out(v):
        def body(j, carry):
            for dest, off in ((gba, 0), (gbb, half)):
                cols = pl.ds(pl.multiple_of(j * tile, tile), tile)
                from_cols = pl.ds(pl.multiple_of(off + j * tile, tile), tile)
                right = ca[v, :, :, from_cols].reshape(steps * tok, tile)
                value = jnp.dot(hid_t[v], right, preferred_element_type=F32).astype(BF16)
                dest[v, :, :, :, cols] = value.reshape(na, nb, rc, tile)
            return carry

        lax.fori_loop(0, half // tile, body, 0)

    def grad_in(v):
        for item in gd_copies(v):
            item.wait_recv()
        for t in range(steps):
            for item in gs_copies(t, v):
                item.wait_recv()
        own = gs_t[v, me_h] if v == 0 else gs_t[v, :, me_l]
        width = nb if v == 0 else na
        own = own.reshape(width * rc, steps * tok)
        dest = p2i0 if v == 0 else p2i1

        def body(j, carry):
            cols = pl.ds(pl.multiple_of(j * tile, tile), tile)
            value = jnp.dot(own, gd[v, :, cols], preferred_element_type=F32)
            for k in range((na if v == 0 else nb) - 1):
                left = gsr[v][k].reshape(width * rc, steps * tok)
                value = value + jnp.dot(left, gdr[v][k, :, cols], preferred_element_type=F32)
            dest[:, :, cols] = value.astype(BF16).reshape(width, rc, tile)
            return carry

        lax.fori_loop(0, wid // tile, body, 0)
        for item in copies_two(2, v):
            item.start()

    def copies_one(which, v):
        base = which * vs + v
        if which == 0:
            return to_dp(
                lambda part: gba.at[v, :, part], lambda k: r1a.at[v, k],
                lambda k: r1_s.at[base, k], lambda k: r1_r.at[base, k], "l",
            )
        return to_dp(
            lambda part: gbb.at[v, part], lambda k: r1b.at[v, k],
            lambda k: r1_s.at[base, k], lambda k: r1_r.at[base, k], "h",
        )

    def copies_two(which, v):
        base = which * vs + v
        if which == 0:
            source, dest, kind = p2a.at[v], r2a.at[v], "h"
        elif which == 1:
            source, dest, kind = p2b.at[v], r2b.at[v], "l"
        elif v == 1:
            source, dest, kind = p2i1, r2i1, "h"
        else:
            source, dest, kind = p2i0, r2i0, "l"
        return to_dp(
            lambda part: source.at[part], lambda k: dest.at[k],
            lambda k: r2_s.at[base, k], lambda k: r2_r.at[base, k], kind,
        )

    def middle(which, v):
        for item in copies_one(which, v):
            item.wait_recv()
        if which == 0:
            total = gba[v, :, me_l].astype(F32)
            for k in range(nb - 1):
                total = total + r1a[v, k].astype(F32)
            p2a[v] = total.astype(BF16)
        else:
            total = gbb[v, me_h].astype(F32)
            for k in range(na - 1):
                total = total + r1b[v, k].astype(F32)
            p2b[v] = total.astype(BF16)
        for item in copies_two(which, v):
            item.start()

    scale = 1.0 / (ndp * tok)

    def final(which, v):
        for item in copies_two(which, v):
            item.wait_recv()
        along_h = which == 0 or (which == 2 and v == 1)
        source = {0: p2a.at[v], 1: p2b.at[v], 2: p2i1 if v == 1 else p2i0}[which]
        got = {0: r2a.at[v], 1: r2b.at[v], 2: r2i1 if v == 1 else r2i0}[which]
        total = source[me_h if along_h else me_l].astype(F32)
        for k in range((na if along_h else nb) - 1):
            total = total + got[k].astype(F32)
        if which == 2:
            fi[v] = total * scale
        else:
            fo[v, :, pl.ds(which * half, half)] = total * scale

    loads[0].wait()
    loads[1].wait()
    back_part(0, 1)
    loads[2].wait()
    prep(1)
    loads[3].wait()
    pre_part(1)
    loads[4].wait()
    prep(0)
    finish_sq(1)
    for item in pre_copies[1]:
        item.wait_recv()
    finish_pre(1, [0])
    finish_back(0, 1)
    send_on(0, 1, 0, 2)
    loads[5].wait()
    loads[6].wait()
    back_part(0, 0)
    loads[7].wait()
    pre_part(0)
    finish_pre(1, range(1, steps))
    finish_sq(0)
    for item in pre_copies[0]:
        item.wait_recv()
    finish_pre(0, [0])
    finish_back(0, 0)
    send_on(0, 0, 0, 2)
    finish_pre(0, range(1, steps))
    loads[8].wait()
    for item in stat_copies:
        item.wait_recv()
    for t in range(1, steps):
        for v in (1, 0):
            take(t, v)
            back_part(t, v)
            if t == steps - 1:
                grad_out(v)
            finish_back(t, v)
            if t < steps - 1:
                send_on(t, v, 0, 2)
            elif v == 1:
                grad_in(1)
    middle(0, 1)
    middle(1, 1)
    grad_in(0)
    middle(0, 0)
    middle(1, 0)
    for v in (1, 0):
        for which in (2, 0, 1):
            final(which, v)
    for item in stat_copies + sq_copies(0) + sq_copies(1):
        item.wait_send()
    for v in range(vs):
        for item in pre_copies[v] + gd_copies(v):
            item.wait_send()
        for t in range(steps):
            for item in back_copies[t, v] + gs_copies(t, v):
                item.wait_send()
            if t < steps - 1:
                sent_on(t, v)
        for item in copies_one(0, v) + copies_one(1, v):
            item.wait_send()
        for which in range(3):
            for item in copies_two(which, v):
                item.wait_send()


def shards(
    saved_inputs, proj_in, proj_out, norm_gain, arriving, logp_grad, rewards, seq_lengths, group_ids
):
    nt = lax.axis_size("tensor")
    npipe = lax.axis_size("pipe")
    ndp = lax.axis_size("dp")
    steps, vs, _, tok, wid = saved_inputs.shape
    rank = proj_in.shape[2]
    new_count = logp_grad.shape[0]
    group_count = new_count * ndp * rewards.shape[2] // 8
    lanes = -(-(group_count + 1) // 128) * 128
    na, nb = factors(ndp)
    rc = rank // ndp
    half = wid // 2
    hm, lm = max(na - 1, 1), max(nb - 1, 1)
    dims = (steps, vs, tok, wid, rank, nt, npipe, ndp)
    peers = max(nt - 1, 1)
    any_spec = pl.BlockSpec(memory_space=pl.ANY)
    vmem = pl.BlockSpec(memory_space=pltpu.VMEM)
    V = pltpu.VMEM
    DMA = pltpu.SemaphoreType.DMA
    pmax = max(na, nb)
    smem = pl.BlockSpec(memory_space=pltpu.SMEM)
    scratch = [
        V((steps, vs, tok, wid), BF16),
        V((vs, steps * tok, wid), BF16),
        V((vs, steps, tok, wid), BF16),
        V((vs, rank, wid), BF16),
        V((vs, rank, wid), BF16),
        V((new_count, tok, wid), BF16),
        V((vs, steps * tok, rank), BF16),
        V((peers, vs, steps * tok, rank), BF16),
        V((vs, steps * tok, rank), F32),
        V((vs, steps * tok, rank), F32),
        V((vs, rank, steps * tok), BF16),
        V((vs, steps * tok, rank), BF16),
        V((vs, na, nb, rc, steps * tok), BF16),
        V((hm, nb, rc, steps * tok), BF16),
        V((lm, na, rc, steps * tok), BF16),
        V((hm, steps * tok, wid), BF16),
        V((lm, steps * tok, wid), BF16),
        V((vs, steps, tok, rank), BF16),
        V((peers, vs, steps, tok, rank), BF16),
        V((steps - 1, vs, tok, wid), BF16),
        V((vs, tok, 128), F32),
        V((peers, vs, tok, 128), F32),
        V((vs, tok, 128), F32),
        V((8, lanes), F32),
        V((max(ndp - 1, 1), 8, lanes), F32),
        V((vs, na, nb, rc, half), BF16),
        V((vs, na, nb, rc, half), BF16),
        V((vs, lm, na, rc, half), BF16),
        V((vs, hm, nb, rc, half), BF16),
        V((vs, na, rc, half), BF16),
        V((vs, nb, rc, half), BF16),
        V((vs, hm, rc, half), BF16),
        V((vs, lm, rc, half), BF16),
        V((nb, rc, wid), BF16),
        V((na, rc, wid), BF16),
        V((lm, rc, wid), BF16),
        V((hm, rc, wid), BF16),
        DMA((9,)),
        DMA((2, vs, peers)),
        DMA((2, max(ndp - 1, 1))),
        DMA((2, vs, peers)),
        DMA((2, vs * steps, peers)),
        DMA((steps - 1, vs, 2)),
        DMA((steps - 1, vs, 2)),
        DMA((vs, pmax)),
        DMA((vs, pmax)),
        DMA((vs * steps, pmax)),
        DMA((vs * steps, pmax)),
        DMA((2 * vs, pmax)),
        DMA((2 * vs, pmax)),
        DMA((3 * vs, pmax)),
        DMA((3 * vs, pmax)),
    ]
    grad_in, grad_out, leaving = pl.pallas_call(
        functools.partial(kernel, dims),
        out_shape=(
            V((vs, rc, wid), F32),
            V((vs, rc, wid), F32),
            V((vs, tok, wid), BF16),
        ),
        in_specs=[any_spec, any_spec, any_spec, vmem, any_spec, any_spec, smem, smem, smem],
        out_specs=(vmem, vmem, vmem),
        scratch_shapes=scratch,
        compiler_params=pltpu.CompilerParams(
            collective_id=0, has_side_effects=True, vmem_limit_bytes=56 * 1024 * 1024
        ),
    )(
        saved_inputs[:, :, 0], proj_in[:, 0], proj_out[:, 0], norm_gain, arriving[:, 0], logp_grad,
        rewards, seq_lengths, group_ids,
    )
    return grad_in[:, None], grad_out[:, None], leaving[:, None]


def solution(mesh):
    return jax.shard_map(
        shards,
        mesh=mesh,
        in_specs=(
            P(None, None, "pipe", "dp", "tensor"),
            P(None, "pipe", None, "tensor"),
            P(None, "pipe", None, "tensor"),
            P(None, "pipe", "tensor"),
            P(None, "pipe", "dp", "tensor"),
            P(None, "dp", "tensor"),
            P(None, "dp", None),
            P(None, "dp", None),
            P(None, "dp", None),
        ),
        out_specs=(
            P(None, "pipe", "dp", "tensor"),
            P(None, "pipe", "dp", "tensor"),
            P(None, "pipe", "dp", "tensor"),
        ),
        check_vma=False,
    )
```

profile of v0, /device:TPU:0, one launch (start us, length us, event | category | flops | bytes accessed | tf_op | source)
XLA Modules:
  0.0 102.8 jit_solution(17753285049128559747)
XLA Ops:
  0.6 98.6 %shard_map.112 = (f32[2,128,2048]{2,1,0:T(8,128)S(1)}, f32[2,128,2048]{2,1,0:T(8,128)S(1)}, bf16[2,128,2048]{2,1,0:T(8,128)(2,1)S(1)}) custom-call(bf16[3,2,128,2048]{3,2,1,0:T(8,128)(2,1)} %bitcast.18, bf16[2,512,2048]{2,1,0:T(8,128)(2,1)} %bitcast.16, bf16[2,512,2048]{2,1,0:T(8,128)(2,1)} %bitcast.17, f32[2,1,2048]{2,1,0:T(1,128)} %gn_ref.1, ...), custom_call_target="tpu_custom_call" | custom-call | tf_op jit(solution)/shard_map/pallas_call | solution.py:553
  99.2 1.3 %copy.18 = f32[2,1,128,2048]{3,2,1,0:T(8,128)} copy(f32[2,1,128,2048]{3,2,1,0:T(8,128)S(1)} %bitcast.14) | data formatting | bytes 4194304
  100.5 1.3 %copy.19 = f32[2,1,128,2048]{3,2,1,0:T(8,128)} copy(f32[2,1,128,2048]{3,2,1,0:T(8,128)S(1)} %bitcast.13) | data formatting | bytes 4194304
  101.8 1.0 copy.20
where the time goes:
time: 103 us
  Pallas kernels  98.6 us (96%)
  local copies, waits for them, and re-layouts  3.61 us (4%)
    pallas_call x1, Pallas kernels, shards(): pl.pallas_call(functools.partial(kernel, dims), out_shape=(V((vs, rc, wid...  98.6 us
    unnamed x3, local copies, waits for them, and re-layouts  3.61 us

commit v1 on v0

v1 whole, which is shorter than its diff:
```python
import functools

import jax
import jax.numpy as jnp
from jax import lax
from jax.experimental import pallas as pl
from jax.experimental.pallas import tpu as pltpu
from jax.sharding import PartitionSpec as P

EPS = 1e-05
MESH = pl.DeviceIdType.MESH
F32 = jnp.float32
BF16 = jnp.bfloat16


def dot_nt(a, b):
    return lax.dot_general(a, b, (((1,), (1,)), ((), ())), preferred_element_type=F32)


def factors(n):
    low = 1
    for k in range(1, n + 1):
        if n % k == 0 and k * k <= n:
            low = k
    return low, n // low


CHUNKS = 4
GATHERED = (4, 4)
PARTS = 2
scope = jax.named_scope


def reductions():
    jobs = [("out", v, j) for v in (1, 0) for j in range(CHUNKS)]
    jobs += [("in", v, j) for v in (1, 0) for j in range(GATHERED[v], CHUNKS)]
    return {job: e for e, job in enumerate(jobs)}


def kernel(
    dims,
    x_hbm, wi_hbm, wo_hbm, gn_hbm, ar_hbm, lp_hbm, rew_hbm, len_hbm, ids_hbm,
    fi, fo, lv,
    xs, gd, ca, wi, wo, lp, ps, pr, presum, slope, hid_t, gs, gs_t, gsr0, gsr1, xr0, xr1, bs, br, ob,
    sqs, sqr, inv_t, stl, str_, gb, r1, p2, r2, p2i, r2i,
    gn_ref, rew_ref, len_ref, ids_ref, str2,
    in_sem, sq_sem, st_sem, pre_sem, back_sem, pipe_s, pipe_r, xg_s, xg_r, gt_s, gt_r,
    r1_s, r1_r, r2_s, r2_r, ri_s, ri_r,
):
    steps, vs, tok, wid, rank, nt, npipe, ndp = dims
    na, nb = factors(ndp)
    rc = rank // ndp
    full = wid * nt
    tile = min(512, wid // 2)
    rtile = min(512, rank)
    cc = wid // CHUNKS
    part_tok = tok // PARTS
    lanes = stl.shape[2]
    new_count, _, seq_count = rew_ref.shape
    unit_lane = new_count * ndp * seq_count // 8
    me_t = lax.axis_index("tensor")
    me_p = lax.axis_index("pipe")
    me_d = lax.axis_index("dp")
    me_h = me_d // nb
    me_l = me_d % nb
    prev_p = lax.rem(me_p + npipe - 1, npipe)
    next_p = lax.rem(me_p + 1, npipe)

    def load(src, dst, k):
        return pltpu.make_async_copy(src, dst, in_sem.at[k])

    loads = [
        load(ar_hbm.at[1], ca.at[1, 0], 0),
        load(wo_hbm.at[1], wo.at[1], 1),
        load(x_hbm.at[:, 1], xs.at[:, 1], 2),
        load(wi_hbm.at[1], wi.at[1], 3),
        load(x_hbm.at[:, 0], xs.at[:, 0], 4),
        load(ar_hbm.at[0], ca.at[0, 0], 5),
        load(wo_hbm.at[0], wo.at[0], 6),
        load(wi_hbm.at[0], wi.at[0], 7),
        load(lp_hbm, lp, 8),
    ]
    small = [
        load(gn_hbm, gn_ref, 9),
        load(rew_hbm, rew_ref, 10),
        load(len_hbm, len_ref, 11),
        load(ids_hbm, ids_ref, 12),
    ]

    barrier = pltpu.get_barrier_semaphore()
    for k in range(1, nt):
        pl.semaphore_signal(barrier, inc=1, device_id={"tensor": lax.rem(me_t + k, nt)}, device_id_type=MESH)
    for k in range(1, na):
        peer = lax.rem(me_h + k, na) * nb + me_l
        pl.semaphore_signal(barrier, inc=1, device_id={"dp": peer}, device_id_type=MESH)
    for k in range(1, nb):
        peer = me_h * nb + lax.rem(me_l + k, nb)
        pl.semaphore_signal(barrier, inc=1, device_id={"dp": peer}, device_id_type=MESH)
    for other in (prev_p, next_p):
        pl.semaphore_signal(barrier, inc=1, device_id={"pipe": other}, device_id_type=MESH)

    for item in small + loads:
        item.start()

    with scope("barrier"):
        pl.semaphore_wait(barrier, nt - 1 + na - 1 + nb - 1 + 2)

    def to_tensor(src, dst_of, send_of, recv_of):
        return [
            pltpu.make_async_remote_copy(
                src_ref=src, dst_ref=dst_of(k - 1), send_sem=send_of(k - 1), recv_sem=recv_of(k - 1),
                device_id={"tensor": lax.rem(me_t + k, nt)}, device_id_type=MESH,
            )
            for k in range(1, nt)
        ]

    def to_dp(src_of, dst_of, send_of, recv_of, kind):
        out = []
        count = {"h": na, "l": nb}[kind]
        for k in range(1, count):
            if kind == "h":
                part = lax.rem(me_h + k, na)
                who = part * nb + me_l
            else:
                part = lax.rem(me_l + k, nb)
                who = me_h * nb + part
            out.append(
                pltpu.make_async_remote_copy(
                    src_ref=src_of(part), dst_ref=dst_of(k - 1), send_sem=send_of(k - 1), recv_sem=recv_of(k - 1),
                    device_id={"dp": who}, device_id_type=MESH,
                )
            )
        return out

    gather_kind = ("h", "l")
    split_kind = ("l", "h")
    count_of = {"h": na, "l": nb}
    xr = (xr0, xr1)
    gsr = (gsr0, gsr1)

    def x_copies(t, v):
        base = v * steps + t
        cols = pl.ds(0, GATHERED[v] * cc)
        return to_dp(
            lambda part: x_hbm.at[t, v, :, cols], lambda k: xr[v].at[k, t],
            lambda k: xg_s.at[base, k], lambda k: xg_r.at[base, k], gather_kind[v],
        )


    def stat_copies(kind):
        if kind == "l":
            return to_dp(lambda part: stl.at[0], lambda k: str_.at[k], lambda k: st_sem.at[0, k], lambda k: st_sem.at[1, k], kind)
        return to_dp(lambda part: stl.at[1], lambda k: str2.at[k], lambda k: st_sem.at[2, k], lambda k: st_sem.at[3, k], kind)

    def stats_first():
        lane8 = lax.broadcasted_iota(jnp.int32, (8, lanes), 1)
        row8 = lax.broadcasted_iota(jnp.int32, (8, lanes), 0)
        stats_own = jnp.where((row8 == 2) & (lane8 == unit_lane), 1.0, 0.0)
        for n in range(new_count):
            for k in range(seq_count):
                value = jnp.where(row8 == 0, rew_ref[n, 0, k], jnp.where(row8 == 1, 1.0, 0.0))
                stats_own = stats_own + jnp.where(lane8 == ids_ref[n, 0, k], value, 0.0)
        stl[0] = stats_own
        for item in stat_copies("l"):
            item.start()

    def stats_second():
        for item in stat_copies("l"):
            item.wait_recv()
        total = stl[0]
        for k in range(nb - 1):
            total = total + str_[k]
        stl[1] = total
        for item in stat_copies("h"):
            item.start()

    def start_gather(v, which):
        for t in which:
            for item in x_copies(t, v):
                item.start()

    lane = lax.broadcasted_iota(jnp.int32, (tok, 128), 1)

    def sq_copies(v):
        return to_tensor(
            sqs.at[v], lambda k: sqr.at[k, v], lambda k: sq_sem.at[0, v, k], lambda k: sq_sem.at[1, v, k]
        )

    def prep(v):
        def body(t, squares_all):
            row = xs[t, v].astype(F32)
            gd[v, pl.ds(pl.multiple_of(t * tok, tok), tok), :] = (row * gn_ref[v]).astype(BF16)
            squares = jnp.sum(row * row, axis=-1, keepdims=True)
            return jnp.where(lane == t, squares, squares_all)

        sqs[v] = lax.fori_loop(0, steps, body, jnp.zeros((tok, 128), F32))
        for item in sq_copies(v):
            item.start()

    def finish_sq(v):
        for item in sq_copies(v):
            item.wait_recv()
        total = sqs[v]
        for k in range(nt - 1):
            total = total + sqr[k, v]
        inv_t[v] = 1.0 / jnp.sqrt(total * (1.0 / full) + EPS)

    def gs_copies(t, v):
        cols = pl.ds(t * tok, tok)
        base = v * steps + t
        source = (lambda part: gs_t.at[v, part, :, :, cols]) if v == 0 else (lambda part: gs_t.at[v, :, part, :, cols])
        return to_dp(
            source, lambda k: gsr[v].at[k, :, :, cols],
            lambda k: gt_s.at[base, k], lambda k: gt_r.at[base, k], gather_kind[v],
        )

    pre_copies = {}
    back_copies = {}

    def pre_part(v):
        def body(j, carry):
            cols = pl.ds(pl.multiple_of(j * rtile, rtile), rtile)
            ps[v, :, cols] = dot_nt(gd[v], wi[v, cols, :]).astype(BF16)
            return carry

        lax.fori_loop(0, rank // rtile, body, 0)
        pre_copies[v] = to_tensor(
            ps.at[v], lambda k: pr.at[k, v], lambda k: pre_sem.at[0, v, k], lambda k: pre_sem.at[1, v, k]
        )
        for item in pre_copies[v]:
            item.start()

    def rows_of(h):
        return pl.ds(h * part_tok, part_tok)

    def back_part(t, v, h=None):
        rows = pl.ds(0, tok) if h is None else rows_of(h)

        def body(j, carry):
            cols = pl.ds(pl.multiple_of(j * rtile, rtile), rtile)
            bs[v, t, rows, cols] = dot_nt(ca[v, t, rows, :], wo[v, cols, :]).astype(BF16)
            return carry

        lax.fori_loop(0, rank // rtile, body, 0)
        base = (v * steps + t) * PARTS + (h or 0)
        back_copies[t, v, h] = to_tensor(
            bs.at[v, t, rows], lambda k: br.at[k, v, t, rows],
            lambda k: back_sem.at[0, base, k], lambda k: back_sem.at[1, base, k],
        )
        for item in back_copies[t, v, h]:
            item.start()

    def finish_pre(v, which_steps):
        for t in which_steps:
            rows = pl.ds(t * tok, tok)
            total = ps[v, rows, :].astype(F32)
            for k in range(nt - 1):
                total = total + pr[k, v, rows, :].astype(F32)
            pre = inv_t[v, :, t:t + 1] * total
            sigma = jax.nn.sigmoid(pre)
            presum[v, rows, :] = total
            hid_t[v, :, rows] = jnp.transpose(pre * sigma).astype(BF16)
            slope[v, rows, :] = sigma * (1.0 + pre * (1.0 - sigma))

    def wait_back(t, v, h=None):
        for item in back_copies[t, v, h]:
            item.wait_recv()

    def finish_back(t, v, h):
        own = rows_of(h)
        rows = pl.ds(t * tok + h * part_tok, part_tok)
        inv = inv_t[v, own, t:t + 1]
        total = bs[v, t, own, :].astype(F32)
        for k in range(nt - 1):
            total = total + br[k, v, t, own, :].astype(F32)
        grad_pre = total * slope[v, rows, :]
        gs[v, rows, :] = (inv * grad_pre).astype(BF16)
        radial = jnp.sum(grad_pre * presum[v, rows, :], axis=-1, keepdims=True)
        coef = inv * inv * inv * radial * (1.0 / full)

        def body(j, carry):
            cols = pl.ds(pl.multiple_of(j * tile, tile), tile)
            lifted = jnp.dot(gs[v, rows, :], wi[v, :, cols], preferred_element_type=F32)
            out = (
                ca[v, t, own, cols].astype(F32)
                + gn_ref[v, :, cols] * lifted
                - xs[t, v, own, cols].astype(F32) * coef
            ).astype(BF16)
            if t < steps - 1:
                ob[t, v, own, cols] = out
            else:
                lv[v, own, cols] = out
            return carry

        lax.fori_loop(0, wid // tile, body, 0)

    def finish_gs(t, v):
        rows = pl.ds(t * tok, tok)
        flipped = jnp.transpose(gs[v, rows, :].astype(F32)).astype(BF16)
        gs_t[v, :, :, :, rows] = flipped.reshape(na, nb, rc, tok)
        for item in gs_copies(t, v):
            item.start()

    def pipe_copy(t, v, slot, h):
        return pltpu.make_async_remote_copy(
            src_ref=ob.at[t, v, rows_of(h)], dst_ref=ca.at[slot, t + 1, rows_of(h)],
            send_sem=pipe_s.at[t, v, h], recv_sem=pipe_r.at[t, slot, h],
            device_id={"pipe": prev_p}, device_id_type=MESH,
        )

    def send_on(t, v, h):
        @pl.when(me_p > 0)
        def _():
            pipe_copy(t, v, v, h).start()

        if v == 1:
            @pl.when(me_p == 0)
            def _():
                pipe_copy(t, 1, 0, h).start()

    def sent_on(t, v, h):
        @pl.when(me_p > 0)
        def _():
            pipe_copy(t, v, v, h).wait_send()

        if v == 1:
            @pl.when(me_p == 0)
            def _():
                pipe_copy(t, 1, 0, h).wait_send()

    def take(t, v, h):
        if v == 0:
            pipe_copy(t - 1, v, v, h).wait_recv()
        else:
            @pl.when(me_p < npipe - 1)
            def _():
                pipe_copy(t - 1, v, v, h).wait_recv()

            @pl.when(me_p == npipe - 1)
            def _():
                stats = stl[1]
                for k in range(na - 1):
                    stats = stats + str2[k]
                means = stats[0:1] / jnp.maximum(stats[1:2], 1.0) + stats[2:3] * (1.0 / ndp)
                tok_row = lax.broadcasted_iota(jnp.int32, (part_tok, lanes), 0) + h * part_tok
                tok_lane = lax.broadcasted_iota(jnp.int32, (part_tok, lanes), 1)
                hot = jnp.zeros((part_tok, lanes), F32)
                begin = 0
                for k in range(seq_count):
                    finish = begin + len_ref[t - 1, 0, k]
                    inside = (tok_row >= begin) & (tok_row < finish)
                    value = jnp.where(tok_lane == ids_ref[t - 1, 0, k], 1.0, 0.0)
                    value = value - jnp.where(tok_lane == unit_lane, rew_ref[t - 1, 0, k], 0.0)
                    hot = hot + jnp.where(inside, value, 0.0)
                    begin = finish
                weight = jnp.sum(hot * means, axis=-1, keepdims=True)
                ca[1, t, rows_of(h), :] = (weight * lp[t - 1, rows_of(h), :].astype(F32)).astype(BF16)

    jobs = reductions()

    def axes_of(job):
        return ("l", "h") if job[2] % 2 == 0 else ("h", "l")

    def cols_of(j):
        return pl.ds(j * cc, cc)

    def split_copies(job):
        e = jobs[job]
        first, second = axes_of(job)
        count = count_of[second]
        source = (lambda part: gb.at[e, :, part]) if first == "l" else (lambda part: gb.at[e, part])
        return to_dp(
            source, lambda k: r1.at[e, k, pl.ds(0, count)], lambda k: r1_s.at[e, k], lambda k: r1_r.at[e, k], first
        )

    def join_copies(job):
        e = jobs[job]
        return to_dp(
            lambda part: p2.at[e, part], lambda k: r2.at[e, k], lambda k: r2_s.at[e, k], lambda k: r2_r.at[e, k],
            axes_of(job)[1],
        )

    def product(job):
        what, v, j = job
        e = jobs[job]
        if what == "out":
            value = jnp.dot(
                hid_t[v], ca[v, :, :, cols_of(j)].reshape(steps * tok, cc), preferred_element_type=F32
            )
        else:
            value = jnp.dot(
                gs_t[v].reshape(rank, steps * tok), xs[:, v, :, cols_of(j)].reshape(steps * tok, cc),
                preferred_element_type=F32,
            ) * gn_ref[v, :, cols_of(j)]
        gb[e] = value.astype(BF16).reshape(na, nb, rc, cc)
        for item in split_copies(job):
            item.start()

    def middle(job):
        e = jobs[job]
        first, second = axes_of(job)
        count = count_of[second]
        for item in split_copies(job):
            item.wait_recv()
        own = gb[e, :, me_l] if first == "l" else gb[e, me_h]
        total = own.astype(F32)
        for k in range(count_of[first] - 1):
            total = total + r1[e, k, :count].astype(F32)
        p2[e, :count] = total.astype(BF16)
        for item in join_copies(job):
            item.start()

    scale = 1.0 / (ndp * tok)

    def final(job):
        what, v, j = job
        e = jobs[job]
        kind = axes_of(job)[1]
        for item in join_copies(job):
            item.wait_recv()
        total = p2[e, me_h if kind == "h" else me_l].astype(F32)
        for k in range(count_of[kind] - 1):
            total = total + r2[e, k].astype(F32)
        dest = fo if what == "out" else fi
        dest[v, :, cols_of(j)] = total * scale

    def in_copies(v, j):
        base = v * CHUNKS + j
        return to_dp(
            lambda part: p2i.at[v, j, part], lambda k: r2i.at[v, j, k],
            lambda k: ri_s.at[base, k], lambda k: ri_r.at[base, k], split_kind[v],
        )

    def wait_gathered(v):
        for t in range(steps):
            for item in x_copies(t, v) + gs_copies(t, v):
                item.wait_recv()

    def grad_in(v, which):
        width = count_of[split_kind[v]]
        own = gs_t[v, me_h] if v == 0 else gs_t[v, :, me_l]
        own = own.reshape(width * rc, steps * tok)
        for j in which:
            value = jnp.dot(
                own, xs[:, v, :, cols_of(j)].reshape(steps * tok, cc), preferred_element_type=F32
            )
            for k in range(count_of[gather_kind[v]] - 1):
                left = gsr[v][k].reshape(width * rc, steps * tok)
                value = value + jnp.dot(
                    left, xr[v][k, :, :, cols_of(j)].reshape(steps * tok, cc), preferred_element_type=F32
                )
            value = value * gn_ref[v, :, cols_of(j)]
            p2i[v, j, :width] = value.astype(BF16).reshape(width, rc, cc)
            for item in in_copies(v, j):
                item.start()

    def final_in(v, j):
        for item in in_copies(v, j):
            item.wait_recv()
        along_h = split_kind[v] == "h"
        total = p2i[v, j, me_h if along_h else me_l].astype(F32)
        for k in range(count_of[split_kind[v]] - 1):
            total = total + r2i[v, j, k].astype(F32)
        fi[v, :, cols_of(j)] = total * scale

    def step(t, v, h):
        with scope(f"take_{t}{v}{h}"):
            take(t, v, h)
        with scope(f"back_{t}{v}{h}"):
            back_part(t, v, h)
            wait_back(t, v, h)
        with scope(f"fin_{t}{v}{h}"):
            finish_back(t, v, h)
        if t < steps - 1 and v == 1:
            send_on(t, v, h)

    halves = range(PARTS)
    with scope("stats"):
        for item in small:
            item.wait()
        start_gather(0, [0])
        stats_first()
        start_gather(1, range(steps))
    with scope("ld01"):
        loads[0].wait()
        loads[1].wait()
    with scope("first1"):
        back_part(0, 1)
        loads[2].wait()
        prep(1)
        loads[3].wait()
        pre_part(1)
        loads[4].wait()
        prep(0)
    with scope("wpre1"):
        finish_sq(1)
        for item in pre_copies[1]:
            item.wait_recv()
    with scope("fin1"):
        finish_pre(1, [0])
        wait_back(0, 1)
        for h in halves:
            finish_back(0, 1, h)
            send_on(0, 1, h)
        finish_gs(0, 1)
    with scope("first0"):
        stats_second()
        start_gather(0, range(1, steps))
        loads[5].wait()
        loads[6].wait()
        back_part(0, 0)
        loads[7].wait()
        pre_part(0)
        finish_pre(1, range(1, steps))
    with scope("wpre0"):
        finish_sq(0)
        for item in pre_copies[0]:
            item.wait_recv()
    with scope("fin0"):
        finish_pre(0, [0])
        wait_back(0, 0)
        for h in halves:
            finish_back(0, 0, h)
        finish_gs(0, 0)
        finish_pre(0, range(1, steps))
        loads[8].wait()
        for item in stat_copies("h"):
            item.wait_recv()

    for t in range(1, steps):
        for h in halves:
            step(t, 1, h)
        if t < steps - 1:
            if t == 1:
                for h in halves:
                    send_on(0, 0, h)
            finish_gs(t, 1)
    with scope("gout1"):
        finish_gs(steps - 1, 1)
        for j in range(CHUNKS):
            product(("out", 1, j))
    for t in range(1, steps - 1):
        for h in halves:
            step(t, 0, h)
            send_on(t, 0, h)
        finish_gs(t, 0)
    with scope("wgat1"):
        wait_gathered(1)
    with scope("gin1"):
        grad_in(1, range(GATHERED[1]))
    for j in range(GATHERED[1], CHUNKS):
        product(("in", 1, j))
    t = steps - 1
    step(t, 0, 0)
    with scope("mid1a"):
        for j in range(CHUNKS):
            middle(("out", 1, j))
    for h in halves[1:]:
        step(t, 0, h)
    with scope("gout0"):
        finish_gs(t, 0)
        for j in range(CHUNKS):
            product(("out", 0, j))
    with scope("mid1b"):
        for j in range(GATHERED[1], CHUNKS):
            middle(("in", 1, j))
    with scope("wgat0"):
        wait_gathered(0)
    with scope("gin0"):
        grad_in(0, range(GATHERED[0]))
        for j in range(GATHERED[0], CHUNKS):
            product(("in", 0, j))
    with scope("final1i"):
        for j in range(GATHERED[1]):
            final_in(1, j)
    for j in range(CHUNKS):
        with scope(f"mid0_{j}"):
            middle(("out", 0, j))
    for j in range(GATHERED[0], CHUNKS):
        middle(("in", 0, j))
    with scope("final1"):
        for job in jobs:
            if job[1] == 1:
                final(job)
    with scope("final0i"):
        for j in range(GATHERED[0]):
            final_in(0, j)
    for job in jobs:
        if job[1] == 0:
            with scope(f"fin0_{job[2]}"):
                final(job)
    for item in stat_copies("l") + stat_copies("h") + sq_copies(0) + sq_copies(1):
        item.wait_send()
    for items in back_copies.values():
        for item in items:
            item.wait_send()
    for v in range(vs):
        for item in pre_copies[v]:
            item.wait_send()
        for t in range(steps):
            for item in x_copies(t, v) + gs_copies(t, v):
                item.wait_send()
            if t < steps - 1:
                for h in halves:
                    sent_on(t, v, h)
        for j in range(GATHERED[v]):
            for item in in_copies(v, j):
                item.wait_send()
    for job in jobs:
        for item in split_copies(job) + join_copies(job):
            item.wait_send()


def shards(
    saved_inputs, proj_in, proj_out, norm_gain, arriving, logp_grad, rewards, seq_lengths, group_ids
):
    nt = lax.axis_size("tensor")
    npipe = lax.axis_size("pipe")
    ndp = lax.axis_size("dp")
    steps, vs, _, tok, wid = saved_inputs.shape
    rank = proj_in.shape[2]
    new_count = logp_grad.shape[0]
    group_count = new_count * ndp * rewards.shape[2] // 8
    lanes = -(-(group_count + 1) // 128) * 128
    na, nb = factors(ndp)
    rc = rank // ndp
    cc = wid // CHUNKS
    jobs = len(reductions())
    hm, lm = max(na - 1, 1), max(nb - 1, 1)
    dims = (steps, vs, tok, wid, rank, nt, npipe, ndp)
    peers = max(nt - 1, 1)
    any_spec = pl.BlockSpec(memory_space=pl.ANY)
    vmem = pl.BlockSpec(memory_space=pltpu.VMEM)
    V = pltpu.VMEM
    DMA = pltpu.SemaphoreType.DMA
    pmax = max(na, nb)
    less = max(pmax - 1, 1)
    scratch = [
        V((steps, vs, tok, wid), BF16),
        V((vs, steps * tok, wid), BF16),
        V((vs, steps, tok, wid), BF16),
        V((vs, rank, wid), BF16),
        V((vs, rank, wid), BF16),
        V((new_count, tok, wid), BF16),
        V((vs, steps * tok, rank), BF16),
        V((peers, vs, steps * tok, rank), BF16),
        V((vs, steps * tok, rank), F32),
        V((vs, steps * tok, rank), F32),
        V((vs, rank, steps * tok), BF16),
        V((vs, steps * tok, rank), BF16),
        V((vs, na, nb, rc, steps * tok), BF16),
        V((hm, nb, rc, steps * tok), BF16),
        V((lm, na, rc, steps * tok), BF16),
        V((hm, steps, tok, GATHERED[0] * cc), BF16),
        V((lm, steps, tok, GATHERED[1] * cc), BF16),
        V((vs, steps, tok, rank), BF16),
        V((peers, vs, steps, tok, rank), BF16),
        V((steps - 1, vs, tok, wid), BF16),
        V((vs, tok, 128), F32),
        V((peers, vs, tok, 128), F32),
        V((vs, tok, 128), F32),
        V((2, 8, lanes), F32),
        V((lm, 8, lanes), F32),
        V((jobs, na, nb, rc, cc), BF16),
        V((jobs, less, pmax, rc, cc), BF16),
        V((jobs, pmax, rc, cc), BF16),
        V((jobs, less, rc, cc), BF16),
        V((vs, CHUNKS, pmax, rc, cc), BF16),
        V((vs, CHUNKS, less, rc, cc), BF16),
        V(norm_gain.shape, F32),
        pltpu.SMEM(rewards.shape, F32),
        pltpu.SMEM(seq_lengths.shape, jnp.int32),
        pltpu.SMEM(group_ids.shape, jnp.int32),
        V((hm, 8, lanes), F32),
        DMA((13,)),
        DMA((2, vs, peers)),
        DMA((4, less)),
        DMA((2, vs, peers)),
        DMA((2, vs * steps * PARTS, peers)),
        DMA((steps - 1, vs, PARTS)),
        DMA((steps - 1, vs, PARTS)),
        DMA((vs * steps, less)),
        DMA((vs * steps, less)),
        DMA((vs * steps, less)),
        DMA((vs * steps, less)),
        DMA((jobs, less)),
        DMA((jobs, less)),
        DMA((jobs, less)),
        DMA((jobs, less)),
        DMA((vs * CHUNKS, less)),
        DMA((vs * CHUNKS, less)),
    ]
    grad_in, grad_out, leaving = pl.pallas_call(
        functools.partial(kernel, dims),
        out_shape=(
            V((vs, rc, wid), F32),
            V((vs, rc, wid), F32),
            V((vs, tok, wid), BF16),
        ),
        in_specs=[any_spec] * 9,
        out_specs=(vmem, vmem, vmem),
        scratch_shapes=scratch,
        compiler_params=pltpu.CompilerParams(
            collective_id=0, has_side_effects=True, vmem_limit_bytes=58 * 1024 * 1024
        ),
    )(
        saved_inputs[:, :, 0], proj_in[:, 0], proj_out[:, 0], norm_gain, arriving[:, 0], logp_grad,
        rewards, seq_lengths, group_ids,
    )
    return grad_in[:, None], grad_out[:, None], leaving[:, None]


def solution(mesh):
    return jax.shard_map(
        shards,
        mesh=mesh,
        in_specs=(
            P(None, None, "pipe", "dp", "tensor"),
            P(None, "pipe", None, "tensor"),
            P(None, "pipe", None, "tensor"),
            P(None, "pipe", "tensor"),
            P(None, "pipe", "dp", "tensor"),
            P(None, "dp", "tensor"),
            P(None, "dp", None),
            P(None, "dp", None),
            P(None, "dp", None),
        ),
        out_specs=(
            P(None, "pipe", "dp", "tensor"),
            P(None, "pipe", "dp", "tensor"),
            P(None, "pipe", "dp", "tensor"),
        ),
        check_vma=False,
    )
```

time: 103 us -> 97.8 us (0.950)
  Pallas kernels: 98.6 us -> 93.4 us
    pallas_call x1, Pallas kernels: 98.6 us -> 93.4 us  [shards(): pl.pallas_call(functools.partial(kernel, dims), out_shape=(V((vs, rc, wid...]
where the time goes in v1:
time: 97.8 us; the launch traced here: 97.6 us
  Pallas kernels  93.4 us (96%)
  local copies, waits for them, and re-layouts  3.61 us (4%)
    pallas_call x1, Pallas kernels, shards(): pl.pallas_call(functools.partial(kernel, dims), out_shape=(V((vs, rc, wid...  93.4 us
    unnamed x3, local copies, waits for them, and re-layouts  3.61 us

profile of v1, /device:TPU:0, one launch (start us, length us, event | category | flops | bytes accessed | tf_op | source)
XLA Modules:
  0.0 97.6 jit_solution(9016414710863085201)
XLA Ops:
  0.6 93.4 %shard_map.112 = (f32[2,128,2048]{2,1,0:T(8,128)S(1)}, f32[2,128,2048]{2,1,0:T(8,128)S(1)}, bf16[2,128,2048]{2,1,0:T(8,128)(2,1)S(1)}) custom-call(bf16[3,2,128,2048]{3,2,1,0:T(8,128)(2,1)} %bitcast.18, bf16[2,512,2048]{2,1,0:T(8,128)(2,1)} %bitcast.16, bf16[2,512,2048]{2,1,0:T(8,128)(2,1)} %bitcast.17, f32[2,1,2048]{2,1,0:T(1,128)} %gn_hbm.1, ...), custom_call_target="tpu_custom_call" | custom-call | tf_op jit(solution)/shard_map/pallas_call | solution.py:693
  94.0 1.3 %copy.18 = f32[2,1,128,2048]{3,2,1,0:T(8,128)} copy(f32[2,1,128,2048]{3,2,1,0:T(8,128)S(1)} %bitcast.14) | data formatting | bytes 4194304
  95.3 1.3 %copy.19 = f32[2,1,128,2048]{3,2,1,0:T(8,128)} copy(f32[2,1,128,2048]{3,2,1,0:T(8,128)S(1)} %bitcast.13) | data formatting | bytes 4194304
  96.6 1.0 copy.20

commit v2 on v1

--- a/solution.py
+++ b/solution.py
@@ -28,6 +28,7 @@
 CHUNKS = 4
 GATHERED = (4, 4)
 PARTS = 2
+FIRST_AXIS = ("hhhl", "lllh")
 scope = jax.named_scope
 
 
@@ -43,8 +44,8 @@
     fi, fo, lv,
     xs, gd, ca, wi, wo, lp, ps, pr, presum, slope, hid_t, gs, gs_t, gsr0, gsr1, xr0, xr1, bs, br, ob,
     sqs, sqr, inv_t, stl, str_, gb, r1, p2, r2, p2i, r2i,
-    gn_ref, rew_ref, len_ref, ids_ref, str2,
-    in_sem, sq_sem, st_sem, pre_sem, back_sem, pipe_s, pipe_r, xg_s, xg_r, gt_s, gt_r,
+    gn_ref, rew_ref, len_ref, ids_ref, str2, wrap_sem,
+    in_sem, sq_sem, st_sem, pre_sem, back_sem, pipe_s, pipe_r, xg_s, xg_r, gt_s, gt_r, gf_s, gf_r,
     r1_s, r1_r, r2_s, r2_r, ri_s, ri_r,
 ):
     steps, vs, tok, wid, rank, nt, npipe, ndp = dims
@@ -96,14 +97,26 @@
     for k in range(1, nb):
         peer = me_h * nb + lax.rem(me_l + k, nb)
         pl.semaphore_signal(barrier, inc=1, device_id={"dp": peer}, device_id_type=MESH)
-    for other in (prev_p, next_p):
-        pl.semaphore_signal(barrier, inc=1, device_id={"pipe": other}, device_id_type=MESH)
+
+    @pl.when(me_p < npipe - 1)
+    def _():
+        pl.semaphore_signal(barrier, inc=1, device_id={"pipe": next_p}, device_id_type=MESH)
+
+    @pl.when(me_p == 0)
+    def _():
+        pl.semaphore_signal(barrier, inc=1, device_id={"pipe": prev_p}, device_id_type=MESH)
+
 
     for item in small + loads:
         item.start()
 
     with scope("barrier"):
-        pl.semaphore_wait(barrier, nt - 1 + na - 1 + nb - 1 + 2)
+        along_pipe = jnp.where(me_p == 0, 0, jnp.where(me_p == npipe - 1, 2, 1))
+        pl.semaphore_wait(barrier, nt - 1 + na - 1 + nb - 1 + along_pipe)
+
+    @pl.when(me_p == npipe - 1)
+    def _():
+        pl.semaphore_signal(wrap_sem, inc=1, device_id={"pipe": next_p}, device_id_type=MESH)
 
     def to_tensor(src, dst_of, send_of, recv_of):
         return [
@@ -205,14 +218,32 @@
             total = total + sqr[k, v]
         inv_t[v] = 1.0 / jnp.sqrt(total * (1.0 / full) + EPS)
 
+    def share_of(v):
+        count = count_of[split_kind[v]]
+        if count % nt:
+            return pl.ds(0, count)
+        return pl.ds(me_t * (count // nt), count // nt)
+
     def gs_copies(t, v):
         cols = pl.ds(t * tok, tok)
         base = v * steps + t
-        source = (lambda part: gs_t.at[v, part, :, :, cols]) if v == 0 else (lambda part: gs_t.at[v, :, part, :, cols])
+        mine = share_of(v)
+        source = (lambda part: gs_t.at[v, part, mine, :, cols]) if v == 0 else (lambda part: gs_t.at[v, mine, part, :, cols])
         return to_dp(
-            source, lambda k: gsr[v].at[k, :, :, cols],
+            source, lambda k: gsr[v].at[k, mine, :, cols],
             lambda k: gt_s.at[base, k], lambda k: gt_r.at[base, k], gather_kind[v],
         )
+
+    def pass_copies(t, v):
+        if count_of[split_kind[v]] % nt:
+            return []
+        cols = pl.ds(t * tok, tok)
+        base = v * steps + t
+        out = []
+        for k in range(count_of[gather_kind[v]] - 1):
+            piece = gsr[v].at[k, share_of(v), :, cols]
+            out += to_tensor(piece, lambda i: piece, lambda i: gf_s.at[base, k, i], lambda i: gf_r.at[base, k, i])
+        return out
 
     pre_copies = {}
     back_copies = {}
@@ -316,6 +347,8 @@
         if v == 1:
             @pl.when(me_p == 0)
             def _():
+                if t == 0 and h == 0:
+                    pl.semaphore_wait(wrap_sem, 1)
                 pipe_copy(t, 1, 0, h).start()
 
     def sent_on(t, v, h):
@@ -338,6 +371,9 @@
 
             @pl.when(me_p == npipe - 1)
             def _():
+                if t == 1 and h == 0:
+                    for item in stat_copies("h"):
+                        item.wait_recv()
                 stats = stl[1]
                 for k in range(na - 1):
                     stats = stats + str2[k]
@@ -359,7 +395,7 @@
     jobs = reductions()
 
     def axes_of(job):
-        return ("l", "h") if job[2] % 2 == 0 else ("h", "l")
+        return ("l", "h") if FIRST_AXIS[job[1]][job[2]] == "l" else ("h", "l")
 
     def cols_of(j):
         return pl.ds(j * cc, cc)
@@ -433,7 +469,12 @@
 
     def wait_gathered(v):
         for t in range(steps):
-            for item in x_copies(t, v) + gs_copies(t, v):
+            for item in gs_copies(t, v):
+                item.wait_recv()
+            for item in pass_copies(t, v):
+                item.start()
+        for t in range(steps):
+            for item in x_copies(t, v) + pass_copies(t, v):
                 item.wait_recv()
 
     def grad_in(v, which):
@@ -524,8 +565,6 @@
         finish_gs(0, 0)
         finish_pre(0, range(1, steps))
         loads[8].wait()
-        for item in stat_copies("h"):
-            item.wait_recv()
 
     for t in range(1, steps):
         for h in halves:
@@ -535,33 +574,43 @@
                 for h in halves:
                     send_on(0, 0, h)
             finish_gs(t, 1)
+    last = steps - 1
+    early = min(3, GATHERED[1])
     with scope("gout1"):
-        finish_gs(steps - 1, 1)
-        for j in range(CHUNKS):
+        finish_gs(last, 1)
+        for j in (0, 3, 1, 2):
             product(("out", 1, j))
-    for t in range(1, steps - 1):
+        for j in range(GATHERED[1], CHUNKS):
+            product(("in", 1, j))
+
+    def gather_in_1():
+        with scope("wgat1"):
+            wait_gathered(1)
+        with scope("gin1"):
+            grad_in(1, range(early))
+
+    for t in range(1, last):
         for h in halves:
             step(t, 0, h)
             send_on(t, 0, h)
+            if t == last - 1 and h == 0:
+                gather_in_1()
         finish_gs(t, 0)
-    with scope("wgat1"):
-        wait_gathered(1)
-    with scope("gin1"):
-        grad_in(1, range(GATHERED[1]))
-    for j in range(GATHERED[1], CHUNKS):
-        product(("in", 1, j))
-    t = steps - 1
-    step(t, 0, 0)
     with scope("mid1a"):
-        for j in range(CHUNKS):
-            middle(("out", 1, j))
+        middle(("out", 1, 3))
+        middle(("out", 1, 0))
+    step(last, 0, 0)
+    with scope("mid1b"):
+        middle(("out", 1, 1))
     for h in halves[1:]:
-        step(t, 0, h)
+        step(last, 0, h)
     with scope("gout0"):
-        finish_gs(t, 0)
-        for j in range(CHUNKS):
+        finish_gs(last, 0)
+        for j in (3, 0, 1, 2):
             product(("out", 0, j))
-    with scope("mid1b"):
+    with scope("gin1b"):
+        middle(("out", 1, 2))
+        grad_in(1, range(early, GATHERED[1]))
         for j in range(GATHERED[1], CHUNKS):
             middle(("in", 1, j))
     with scope("wgat0"):
@@ -570,45 +619,73 @@
         grad_in(0, range(GATHERED[0]))
         for j in range(GATHERED[0], CHUNKS):
             product(("in", 0, j))
-    with scope("final1i"):
-        for j in range(GATHERED[1]):
+    with scope("mid0_3"):
+        middle(("out", 0, 3))
+    with scope("mid0_0"):
+        middle(("out", 0, 0))
+    with scope("final1a"):
+        for j in (0, 1, 3):
+            final(("out", 1, j))
+        for j in range(early):
             final_in(1, j)
-    for j in range(CHUNKS):
+    @pl.when(me_p < npipe - 1)
+    def _():
+        for item in stat_copies("h"):
+            item.wait_recv()
+
+    with scope("drain"):
+        for item in stat_copies("l") + stat_copies("h") + sq_copies(0) + sq_copies(1):
+            item.wait_send()
+        for items in back_copies.values():
+            for item in items:
+                item.wait_send()
+        for v in range(vs):
+            for item in pre_copies[v]:
+                item.wait_send()
+            for t in range(steps):
+                for item in x_copies(t, v) + gs_copies(t, v) + pass_copies(t, v):
+                    item.wait_send()
+                if t < steps - 1:
+                    for h in halves:
+                        sent_on(t, v, h)
+    for j in (1, 2):
         with scope(f"mid0_{j}"):
             middle(("out", 0, j))
     for j in range(GATHERED[0], CHUNKS):
         middle(("in", 0, j))
-    with scope("final1"):
-        for job in jobs:
-            if job[1] == 1:
-                final(job)
     with scope("final0i"):
         for j in range(GATHERED[0]):
             final_in(0, j)
-    for job in jobs:
-        if job[1] == 0:
-            with scope(f"fin0_{job[2]}"):
-                final(job)
-    for item in stat_copies("l") + stat_copies("h") + sq_copies(0) + sq_copies(1):
-        item.wait_send()
-    for items in back_copies.values():
-        for item in items:
-            item.wait_send()
+    with scope("final1b"):
+        for j in range(early, GATHERED[1]):
+            final_in(1, j)
+        for j in range(GATHERED[1], CHUNKS):
+            final(("in", 1, j))
+        final(("out", 1, 2))
     for v in range(vs):
-        for item in pre_copies[v]:
-            item.wait_send()
-        for t in range(steps):
-            for item in x_copies(t, v) + gs_copies(t, v):
-                item.wait_send()
-            if t < steps - 1:
-                for h in halves:
-                    sent_on(t, v, h)
         for j in range(GATHERED[v]):
             for item in in_copies(v, j):
                 item.wait_send()
     for job in jobs:
-        for item in split_copies(job) + join_copies(job):
+        for item in split_copies(job):
             item.wait_send()
+    for j in (0, 1, 3, 2):
+        with scope(f"fin0_{j}"):
+            final(("out", 0, j))
+    for j in range(GATHERED[0], CHUNKS):
+        final(("in", 0, j))
+    with scope("tail"):
+        for job in jobs:
+            for item in join_copies(job):
+                item.wait_send()
+
+
+def store(a, b, c, a_out, b_out, c_out, sem):
+    copies = [pltpu.make_async_copy(*pair, sem.at[k]) for k, pair in enumerate(((a, a_out), (b, b_out), (c, c_out)))]
+    for item in copies:
+        item.start()
+    for item in copies:
+        item.wait()
 
 
 def shards(
@@ -672,6 +749,7 @@
         pltpu.SMEM(seq_lengths.shape, jnp.int32),
         pltpu.SMEM(group_ids.shape, jnp.int32),
         V((hm, 8, lanes), F32),
+        pltpu.SemaphoreType.REGULAR,
         DMA((13,)),
         DMA((2, vs, peers)),
         DMA((4, less)),
@@ -683,6 +761,8 @@
         DMA((vs * steps, less)),
         DMA((vs * steps, less)),
         DMA((vs * steps, less)),
+        DMA((vs * steps, less, peers)),
+        DMA((vs * steps, less, peers)),
         DMA((jobs, less)),
         DMA((jobs, less)),
         DMA((jobs, less)),
@@ -707,6 +787,14 @@
         saved_inputs[:, :, 0], proj_in[:, 0], proj_out[:, 0], norm_gain, arriving[:, 0], logp_grad,
         rewards, seq_lengths, group_ids,
     )
+    grad_in, grad_out, leaving = pl.pallas_call(
+        store,
+        out_shape=tuple(jax.ShapeDtypeStruct(a.shape, a.dtype) for a in (grad_in, grad_out, leaving)),
+        in_specs=[vmem] * 3,
+        out_specs=[any_spec] * 3,
+        scratch_shapes=[DMA((3,))],
+        compiler_params=pltpu.CompilerParams(vmem_limit_bytes=1024 * 1024),
+    )(grad_in, grad_out, leaving)
     return grad_in[:, None], grad_out[:, None], leaving[:, None]
 
 

time: 97.8 us -> 92.6 us (0.947)
  local copies, waits for them, and re-layouts: 3.61 us -> 0 us
  Pallas kernels: 93.4 us -> 91.6 us
    pallas_call x1, Pallas kernels: 93.4 us -> 89.2 us  [shards(): pl.pallas_call(functools.partial(kernel, dims), out_shape=(V((vs, rc, wid...]
    unnamed x3 -> x0, local copies, waits for them, and re-layouts: 3.61 us -> none
    pallas_call x0 -> x1, Pallas kernels: none -> 2.38 us  [shards(): pl.pallas_call(store, out_shape=tuple((jax.ShapeDtypeStruct(a.shape, a.dt...]
where the time goes in v2:
time: 92.6 us; the launch traced here: 92.4 us
  Pallas kernels  91.6 us (99%)
    pallas_call x1, Pallas kernels, shards(): pl.pallas_call(functools.partial(kernel, dims), out_shape=(V((vs, rc, wid...  89.2 us
    pallas_call x1, Pallas kernels, shards(): pl.pallas_call(store, out_shape=tuple((jax.ShapeDtypeStruct(a.shape, a.dt...  2.38 us

profile of v2, /device:TPU:0, one launch (start us, length us, event | category | flops | bytes accessed | tf_op | source)
XLA Modules:
  0.0 92.4 jit_solution(17775512593075102285)
XLA Ops:
  0.6 89.2 %shard_map.112 = (f32[2,128,2048]{2,1,0:T(8,128)S(1)}, f32[2,128,2048]{2,1,0:T(8,128)S(1)}, bf16[2,128,2048]{2,1,0:T(8,128)(2,1)S(1)}) custom-call(bf16[3,2,128,2048]{3,2,1,0:T(8,128)(2,1)} %bitcast.15, bf16[2,512,2048]{2,1,0:T(8,128)(2,1)} %bitcast.13, bf16[2,512,2048]{2,1,0:T(8,128)(2,1)} %bitcast.14, f32[2,1,2048]{2,1,0:T(1,128)} %gn_hbm.1, ...), custom_call_target="tpu_custom_call" | custom-call | tf_op jit(solution)/shard_map/pallas_call | solution.py:773
  89.9 2.4 %shard_map.113 = (f32[2,128,2048]{2,1,0:T(8,128)}, f32[2,128,2048]{2,1,0:T(8,128)}, bf16[2,128,2048]{2,1,0:T(8,128)(2,1)}) custom-call(f32[2,128,2048]{2,1,0:T(8,128)S(1)} %get-tuple-element.9.a, f32[2,128,2048]{2,1,0:T(8,128)S(1)} %get-tuple-element.10.b, bf16[2,128,2048]{2,1,0:T(8,128)(2,1)S(1)} %get-tuple-element.11.c), custom_call_target="tpu_custom_call" | custom-call | tf_op jit(solution)/shard_map/pallas_call | solution.py:790

commit v3 on v2

--- a/solution.py
+++ b/solution.py
@@ -26,9 +26,11 @@
 
 
 CHUNKS = 4
-GATHERED = (4, 4)
+GATHERED = (4, 3)
 PARTS = 2
 FIRST_AXIS = ("hhhl", "lllh")
+IN_AXIS = ("h", "l")
+ORDER = ((3, 0, 1, 2), (3, 0, 1, 2))
 scope = jax.named_scope
 
 
@@ -36,6 +38,15 @@
     jobs = [("out", v, j) for v in (1, 0) for j in range(CHUNKS)]
     jobs += [("in", v, j) for v in (1, 0) for j in range(GATHERED[v], CHUNKS)]
     return {job: e for e, job in enumerate(jobs)}
+
+
+def pieces(steps, t, h):
+    return ORDER[0] if t == steps - 2 and h == PARTS - 1 else (None,)
+
+
+def pipe_slots(steps, vs):
+    keys = [(t, v, h, c) for t in range(steps - 1) for v in range(vs) for h in range(PARTS) for c in pieces(steps, t, h)]
+    return {key: k for k, key in enumerate(keys)}
 
 
 def kernel(
@@ -194,29 +205,35 @@
 
     lane = lax.broadcasted_iota(jnp.int32, (tok, 128), 1)
 
-    def sq_copies(v):
+    groups = ((0, 1), (1, steps))
+
+    def group_of(t):
+        return 0 if t == 0 else 1
+
+    def sq_copies(v, g):
+        base = 2 * v + g
         return to_tensor(
-            sqs.at[v], lambda k: sqr.at[k, v], lambda k: sq_sem.at[0, v, k], lambda k: sq_sem.at[1, v, k]
+            sqs.at[v, g], lambda k: sqr.at[k, v, g], lambda k: sq_sem.at[0, base, k], lambda k: sq_sem.at[1, base, k]
         )
 
-    def prep(v):
+    def prep(v, g):
         def body(t, squares_all):
             row = xs[t, v].astype(F32)
             gd[v, pl.ds(pl.multiple_of(t * tok, tok), tok), :] = (row * gn_ref[v]).astype(BF16)
             squares = jnp.sum(row * row, axis=-1, keepdims=True)
             return jnp.where(lane == t, squares, squares_all)
 
-        sqs[v] = lax.fori_loop(0, steps, body, jnp.zeros((tok, 128), F32))
-        for item in sq_copies(v):
+        sqs[v, g] = lax.fori_loop(*groups[g], body, jnp.zeros((tok, 128), F32))
+        for item in sq_copies(v, g):
             item.start()
 
-    def finish_sq(v):
-        for item in sq_copies(v):
+    def finish_sq(v, g):
+        for item in sq_copies(v, g):
             item.wait_recv()
-        total = sqs[v]
+        total = sqs[v, g]
         for k in range(nt - 1):
-            total = total + sqr[k, v]
-        inv_t[v] = 1.0 / jnp.sqrt(total * (1.0 / full) + EPS)
+            total = total + sqr[k, v, g]
+        inv_t[v, g] = 1.0 / jnp.sqrt(total * (1.0 / full) + EPS)
 
     def share_of(v):
         count = count_of[split_kind[v]]
@@ -248,18 +265,30 @@
     pre_copies = {}
     back_copies = {}
 
-    def pre_part(v):
+    def pre_part(v, g):
+        low, high = groups[g]
+        rows = pl.ds(low * tok, (high - low) * tok)
+
         def body(j, carry):
             cols = pl.ds(pl.multiple_of(j * rtile, rtile), rtile)
-            ps[v, :, cols] = dot_nt(gd[v], wi[v, cols, :]).astype(BF16)
+            ps[v, rows, cols] = dot_nt(gd[v, rows, :], wi[v, cols, :]).astype(BF16)
             return carry
 
         lax.fori_loop(0, rank // rtile, body, 0)
-        pre_copies[v] = to_tensor(
-            ps.at[v], lambda k: pr.at[k, v], lambda k: pre_sem.at[0, v, k], lambda k: pre_sem.at[1, v, k]
+        base = 2 * v + g
+        pre_copies[v, g] = to_tensor(
+            ps.at[v, rows], lambda k: pr.at[k, v, rows], lambda k: pre_sem.at[0, base, k], lambda k: pre_sem.at[1, base, k]
         )
-        for item in pre_copies[v]:
+        for item in pre_copies[v, g]:
             item.start()
+
+    def wait_pre(v, g):
+        finish_sq(v, g)
+        for item in pre_copies[v, g]:
+            item.wait_recv()
+
+    def cols_of(j):
+        return pl.ds(j * cc, cc)
 
     def rows_of(h):
         return pl.ds(h * part_tok, part_tok)
@@ -287,7 +316,7 @@
             total = ps[v, rows, :].astype(F32)
             for k in range(nt - 1):
                 total = total + pr[k, v, rows, :].astype(F32)
-            pre = inv_t[v, :, t:t + 1] * total
+            pre = inv_t[v, group_of(t), :, t:t + 1] * total
             sigma = jax.nn.sigmoid(pre)
             presum[v, rows, :] = total
             hid_t[v, :, rows] = jnp.transpose(pre * sigma).astype(BF16)
@@ -297,10 +326,10 @@
         for item in back_copies[t, v, h]:
             item.wait_recv()
 
-    def finish_back(t, v, h):
+    def finish_back(t, v, h, send=True):
         own = rows_of(h)
         rows = pl.ds(t * tok + h * part_tok, part_tok)
-        inv = inv_t[v, own, t:t + 1]
+        inv = inv_t[v, group_of(t), own, t:t + 1]
         total = bs[v, t, own, :].astype(F32)
         for k in range(nt - 1):
             total = total + br[k, v, t, own, :].astype(F32)
@@ -309,8 +338,7 @@
         radial = jnp.sum(grad_pre * presum[v, rows, :], axis=-1, keepdims=True)
         coef = inv * inv * inv * radial * (1.0 / full)
 
-        def body(j, carry):
-            cols = pl.ds(pl.multiple_of(j * tile, tile), tile)
+        def part(cols):
             lifted = jnp.dot(gs[v, rows, :], wi[v, :, cols], preferred_element_type=F32)
             out = (
                 ca[v, t, own, cols].astype(F32)
@@ -321,9 +349,22 @@
                 ob[t, v, own, cols] = out
             else:
                 lv[v, own, cols] = out
+
+        def body(j, carry):
+            part(pl.ds(pl.multiple_of(j * tile, tile), tile))
             return carry
 
-        lax.fori_loop(0, wid // tile, body, 0)
+        if t < steps - 1 and len(pieces(steps, t, h)) > 1:
+            for c in pieces(steps, t, h):
+                part(cols_of(c))
+                send_on(t, v, h, c)
+        else:
+            lax.fori_loop(0, wid // tile, body, 0)
+            if t < steps - 1 and send:
+                send_on(t, v, h, None)
+
+    halves = range(PARTS)
+    slots = pipe_slots(steps, vs)
 
     def finish_gs(t, v):
         rows = pl.ds(t * tok, tok)
@@ -332,43 +373,53 @@
         for item in gs_copies(t, v):
             item.start()
 
-    def pipe_copy(t, v, slot, h):
+    def pipe_copy(t, v, slot, h, c):
+        where = (rows_of(h),) if c is None else (rows_of(h), cols_of(c))
         return pltpu.make_async_remote_copy(
-            src_ref=ob.at[t, v, rows_of(h)], dst_ref=ca.at[slot, t + 1, rows_of(h)],
-            send_sem=pipe_s.at[t, v, h], recv_sem=pipe_r.at[t, slot, h],
+            src_ref=ob.at[(t, v) + where], dst_ref=ca.at[(slot, t + 1) + where],
+            send_sem=pipe_s.at[slots[t, v, h, c]], recv_sem=pipe_r.at[slots[t, slot, h, c]],
             device_id={"pipe": prev_p}, device_id_type=MESH,
         )
 
-    def send_on(t, v, h):
+    def send_on(t, v, h, c):
         @pl.when(me_p > 0)
         def _():
-            pipe_copy(t, v, v, h).start()
+            pipe_copy(t, v, v, h, c).start()
 
         if v == 1:
             @pl.when(me_p == 0)
             def _():
                 if t == 0 and h == 0:
                     pl.semaphore_wait(wrap_sem, 1)
-                pipe_copy(t, 1, 0, h).start()
+                pipe_copy(t, 1, 0, h, c).start()
 
     def sent_on(t, v, h):
-        @pl.when(me_p > 0)
+        for c in pieces(steps, t, h):
+            @pl.when(me_p > 0)
+            def _():
+                pipe_copy(t, v, v, h, c).wait_send()
+
+            if v == 1:
+                @pl.when(me_p == 0)
+                def _():
+                    pipe_copy(t, 1, 0, h, c).wait_send()
+
+    def take(t, v, h, only=None):
+        want = pieces(steps, t - 1, h)
+        first = only is None or only == want[0]
+        if only is not None:
+            want = (only,)
+        if v == 0:
+            for c in want:
+                pipe_copy(t - 1, v, v, h, c).wait_recv()
+            return
+
+        @pl.when(me_p < npipe - 1)
         def _():
-            pipe_copy(t, v, v, h).wait_send()
-
-        if v == 1:
-            @pl.when(me_p == 0)
-            def _():
-                pipe_copy(t, 1, 0, h).wait_send()
-
-    def take(t, v, h):
-        if v == 0:
-            pipe_copy(t - 1, v, v, h).wait_recv()
-        else:
-            @pl.when(me_p < npipe - 1)
-            def _():
-                pipe_copy(t - 1, v, v, h).wait_recv()
-
+            for c in want:
+                pipe_copy(t - 1, v, v, h, c).wait_recv()
+
+        if first:
             @pl.when(me_p == npipe - 1)
             def _():
                 if t == 1 and h == 0:
@@ -395,10 +446,9 @@
     jobs = reductions()
 
     def axes_of(job):
-        return ("l", "h") if FIRST_AXIS[job[1]][job[2]] == "l" else ("h", "l")
-
-    def cols_of(j):
-        return pl.ds(j * cc, cc)
+        what, v, j = job
+        first = FIRST_AXIS[v][j] if what == "out" else IN_AXIS[v]
+        return ("l", "h") if first == "l" else ("h", "l")
 
     def split_copies(job):
         e = jobs[job]
@@ -504,18 +554,31 @@
             total = total + r2i[v, j, k].astype(F32)
         fi[v, :, cols_of(j)] = total * scale
 
-    def step(t, v, h):
-        with scope(f"take_{t}{v}{h}"):
-            take(t, v, h)
+    last = steps - 1
+
+    def back(t, v, h, during=None):
         with scope(f"back_{t}{v}{h}"):
             back_part(t, v, h)
+            if during is not None:
+                during()
             wait_back(t, v, h)
         with scope(f"fin_{t}{v}{h}"):
             finish_back(t, v, h)
-        if t < steps - 1 and v == 1:
-            send_on(t, v, h)
-
-    halves = range(PARTS)
+
+    def step(t, v, h, during=None):
+        with scope(f"take_{t}{v}{h}"):
+            take(t, v, h)
+        back(t, v, h, during)
+
+    def products(v, which):
+        for j in which:
+            with scope(f"prod_{v}{j}"):
+                take(last, v, PARTS - 1, j)
+                product(("out", v, j))
+
+    def rest(what, v):
+        return range(GATHERED[v], CHUNKS) if what == "in" else range(GATHERED[v])
+
     with scope("stats"):
         for item in small:
             item.wait()
@@ -528,120 +591,129 @@
     with scope("first1"):
         back_part(0, 1)
         loads[2].wait()
-        prep(1)
+        prep(1, 0)
         loads[3].wait()
-        pre_part(1)
+        pre_part(1, 0)
+        prep(1, 1)
         loads[4].wait()
-        prep(0)
+        prep(0, 0)
     with scope("wpre1"):
-        finish_sq(1)
-        for item in pre_copies[1]:
-            item.wait_recv()
+        wait_pre(1, 0)
     with scope("fin1"):
         finish_pre(1, [0])
         wait_back(0, 1)
         for h in halves:
             finish_back(0, 1, h)
-            send_on(0, 1, h)
+    with scope("first0"):
         finish_gs(0, 1)
-    with scope("first0"):
         stats_second()
         start_gather(0, range(1, steps))
+        pre_part(1, 1)
+        prep(0, 1)
         loads[5].wait()
         loads[6].wait()
         back_part(0, 0)
         loads[7].wait()
-        pre_part(0)
+        pre_part(0, 0)
+        pre_part(0, 1)
+        wait_pre(1, 1)
         finish_pre(1, range(1, steps))
     with scope("wpre0"):
-        finish_sq(0)
-        for item in pre_copies[0]:
-            item.wait_recv()
+        wait_pre(0, 0)
     with scope("fin0"):
         finish_pre(0, [0])
         wait_back(0, 0)
         for h in halves:
-            finish_back(0, 0, h)
+            finish_back(0, 0, h, send=False)
         finish_gs(0, 0)
+        wait_pre(0, 1)
         finish_pre(0, range(1, steps))
         loads[8].wait()
 
-    for t in range(1, steps):
+    for t in range(1, last):
         for h in halves:
             step(t, 1, h)
-        if t < steps - 1:
-            if t == 1:
-                for h in halves:
-                    send_on(0, 0, h)
-            finish_gs(t, 1)
-    last = steps - 1
-    early = min(3, GATHERED[1])
+        if t == 1:
+            for h in halves:
+                send_on(0, 0, h, None)
+        finish_gs(t, 1)
+    for h in halves[:-1]:
+        step(last, 1, h)
+    products(1, ORDER[1][:2])
+    for j in ORDER[1][2:]:
+        take(last, 1, PARTS - 1, j)
+    back(last, 1, PARTS - 1)
     with scope("gout1"):
         finish_gs(last, 1)
-        for j in (0, 3, 1, 2):
+        for j in ORDER[1][2:]:
             product(("out", 1, j))
-        for j in range(GATHERED[1], CHUNKS):
+        for j in rest("in", 1):
             product(("in", 1, j))
 
-    def gather_in_1():
-        with scope("wgat1"):
-            wait_gathered(1)
-        with scope("gin1"):
-            grad_in(1, range(early))
+    def first_middles():
+        middle(("out", 1, 0))
 
     for t in range(1, last):
         for h in halves:
-            step(t, 0, h)
-            send_on(t, 0, h)
-            if t == last - 1 and h == 0:
-                gather_in_1()
+            ending = t == last - 1
+            step(t, 0, h, first_middles if ending and h == 0 else None)
+            if ending and h == 0:
+                with scope("wgat1"):
+                    wait_gathered(1)
+                with scope("gin1"):
+                    grad_in(1, rest("out", 1)[:1])
         finish_gs(t, 0)
-    with scope("mid1a"):
+    with scope("mid11"):
+        middle(("out", 1, 1))
         middle(("out", 1, 3))
-        middle(("out", 1, 0))
-    step(last, 0, 0)
-    with scope("mid1b"):
-        middle(("out", 1, 1))
-    for h in halves[1:]:
+    for h in halves[:-1]:
         step(last, 0, h)
+    with scope("mid12"):
+        middle(("out", 1, 2))
+    products(0, ORDER[0][:2])
+    for j in ORDER[0][2:]:
+        take(last, 0, PARTS - 1, j)
+    back(last, 0, PARTS - 1)
     with scope("gout0"):
         finish_gs(last, 0)
-        for j in (3, 0, 1, 2):
+        for j in ORDER[0][2:]:
             product(("out", 0, j))
+        for j in rest("in", 0):
+            product(("in", 0, j))
     with scope("gin1b"):
-        middle(("out", 1, 2))
-        grad_in(1, range(early, GATHERED[1]))
-        for j in range(GATHERED[1], CHUNKS):
+        grad_in(1, rest("out", 1)[1:])
+    with scope("midi1"):
+        for j in rest("in", 1):
             middle(("in", 1, j))
+    with scope("mid0_0"):
+        middle(("out", 0, 0))
     with scope("wgat0"):
         wait_gathered(0)
     with scope("gin0"):
-        grad_in(0, range(GATHERED[0]))
-        for j in range(GATHERED[0], CHUNKS):
-            product(("in", 0, j))
+        grad_in(0, rest("out", 0))
     with scope("mid0_3"):
         middle(("out", 0, 3))
-    with scope("mid0_0"):
-        middle(("out", 0, 0))
     with scope("final1a"):
         for j in (0, 1, 3):
             final(("out", 1, j))
-        for j in range(early):
+        for j in rest("out", 1)[:1]:
             final_in(1, j)
+
     @pl.when(me_p < npipe - 1)
     def _():
         for item in stat_copies("h"):
             item.wait_recv()
 
     with scope("drain"):
-        for item in stat_copies("l") + stat_copies("h") + sq_copies(0) + sq_copies(1):
+        for item in stat_copies("l") + stat_copies("h") + sum([sq_copies(v, g) for v in range(vs) for g in range(2)], []):
             item.wait_send()
         for items in back_copies.values():
             for item in items:
                 item.wait_send()
         for v in range(vs):
-            for item in pre_copies[v]:
-                item.wait_send()
+            for g in range(2):
+                for item in pre_copies[v, g]:
+                    item.wait_send()
             for t in range(steps):
                 for item in x_copies(t, v) + gs_copies(t, v) + pass_copies(t, v):
                     item.wait_send()
@@ -651,15 +723,16 @@
     for j in (1, 2):
         with scope(f"mid0_{j}"):
             middle(("out", 0, j))
-    for j in range(GATHERED[0], CHUNKS):
-        middle(("in", 0, j))
+    with scope("midi0"):
+        for j in rest("in", 0):
+            middle(("in", 0, j))
     with scope("final0i"):
-        for j in range(GATHERED[0]):
+        for j in rest("out", 0):
             final_in(0, j)
     with scope("final1b"):
-        for j in range(early, GATHERED[1]):
+        for j in rest("out", 1)[1:]:
             final_in(1, j)
-        for j in range(GATHERED[1], CHUNKS):
+        for j in rest("in", 1):
             final(("in", 1, j))
         final(("out", 1, 2))
     for v in range(vs):
@@ -672,8 +745,9 @@
     for j in (0, 1, 3, 2):
         with scope(f"fin0_{j}"):
             final(("out", 0, j))
-    for j in range(GATHERED[0], CHUNKS):
-        final(("in", 0, j))
+    with scope("fini0"):
+        for j in rest("in", 0):
+            final(("in", 0, j))
     with scope("tail"):
         for job in jobs:
             for item in join_copies(job):
@@ -703,6 +777,7 @@
     rc = rank // ndp
     cc = wid // CHUNKS
     jobs = len(reductions())
+    pipe_count = len(pipe_slots(steps, vs))
     hm, lm = max(na - 1, 1), max(nb - 1, 1)
     dims = (steps, vs, tok, wid, rank, nt, npipe, ndp)
     peers = max(nt - 1, 1)
@@ -733,9 +808,9 @@
         V((vs, steps, tok, rank), BF16),
         V((peers, vs, steps, tok, rank), BF16),
         V((steps - 1, vs, tok, wid), BF16),
-        V((vs, tok, 128), F32),
-        V((peers, vs, tok, 128), F32),
-        V((vs, tok, 128), F32),
+        V((vs, 2, tok, 128), F32),
+        V((peers, vs, 2, tok, 128), F32),
+        V((vs, 2, tok, 128), F32),
         V((2, 8, lanes), F32),
         V((lm, 8, lanes), F32),
         V((jobs, na, nb, rc, cc), BF16),
@@ -751,12 +826,12 @@
         V((hm, 8, lanes), F32),
         pltpu.SemaphoreType.REGULAR,
         DMA((13,)),
-        DMA((2, vs, peers)),
+        DMA((2, 2 * vs, peers)),
         DMA((4, less)),
-        DMA((2, vs, peers)),
+        DMA((2, 2 * vs, peers)),
         DMA((2, vs * steps * PARTS, peers)),
-        DMA((steps - 1, vs, PARTS)),
-        DMA((steps - 1, vs, PARTS)),
+        DMA((pipe_count,)),
+        DMA((pipe_count,)),
         DMA((vs * steps, less)),
         DMA((vs * steps, less)),
         DMA((vs * steps, less)),

time: 92.6 us -> 91.7 us (level)
  no operation moved by 1% of the time
where the time goes in v3:
time: 91.7 us; the launch traced here: 91.5 us
  Pallas kernels  90.7 us (99%)
    pallas_call x1, Pallas kernels, shards(): pl.pallas_call(functools.partial(kernel, dims), out_shape=(V((vs, rc, wid...  88.4 us
    pallas_call x1, Pallas kernels, shards(): pl.pallas_call(store, out_shape=tuple((jax.ShapeDtypeStruct(a.shape, a.dt...  2.38 us

profile of v3, /device:TPU:0, one launch (start us, length us, event | category | flops | bytes accessed | tf_op | source)
XLA Modules:
  0.0 91.5 jit_solution(5162149478497679115)
XLA Ops:
  0.6 88.4 %shard_map.112 = (f32[2,128,2048]{2,1,0:T(8,128)S(1)}, f32[2,128,2048]{2,1,0:T(8,128)S(1)}, bf16[2,128,2048]{2,1,0:T(8,128)(2,1)S(1)}) custom-call(bf16[3,2,128,2048]{3,2,1,0:T(8,128)(2,1)} %bitcast.15, bf16[2,512,2048]{2,1,0:T(8,128)(2,1)} %bitcast.13, bf16[2,512,2048]{2,1,0:T(8,128)(2,1)} %bitcast.14, f32[2,1,2048]{2,1,0:T(1,128)} %gn_hbm.1, ...), custom_call_target="tpu_custom_call" | custom-call | tf_op jit(solution)/shard_map/pallas_call | solution.py:848
  89.0 2.4 %shard_map.113 = (f32[2,128,2048]{2,1,0:T(8,128)}, f32[2,128,2048]{2,1,0:T(8,128)}, bf16[2,128,2048]{2,1,0:T(8,128)(2,1)}) custom-call(f32[2,128,2048]{2,1,0:T(8,128)S(1)} %get-tuple-element.9.a, f32[2,128,2048]{2,1,0:T(8,128)S(1)} %get-tuple-element.10.b, bf16[2,128,2048]{2,1,0:T(8,128)(2,1)S(1)} %get-tuple-element.11.c), custom_call_target="tpu_custom_call" | custom-call | tf_op jit(solution)/shard_map/pallas_call | solution.py:865

commit v4 on v3

--- a/solution.py
+++ b/solution.py
@@ -26,11 +26,11 @@
 
 
 CHUNKS = 4
-GATHERED = (4, 3)
+GATHERED = (3, 3)
 PARTS = 2
-FIRST_AXIS = ("hhhl", "lllh")
+FIRST_AXIS = ("hhll", "hllh")
 IN_AXIS = ("h", "l")
-ORDER = ((3, 0, 1, 2), (3, 0, 1, 2))
+ORDER = (3, 2, 0, 1)
 scope = jax.named_scope
 
 
@@ -41,7 +41,7 @@
 
 
 def pieces(steps, t, h):
-    return ORDER[0] if t == steps - 2 and h == PARTS - 1 else (None,)
+    return ORDER if (t, h) in ((0, 0), (steps - 2, PARTS - 1)) else (None,)
 
 
 def pipe_slots(steps, vs):
@@ -56,7 +56,7 @@
     xs, gd, ca, wi, wo, lp, ps, pr, presum, slope, hid_t, gs, gs_t, gsr0, gsr1, xr0, xr1, bs, br, ob,
     sqs, sqr, inv_t, stl, str_, gb, r1, p2, r2, p2i, r2i,
     gn_ref, rew_ref, len_ref, ids_ref, str2, wrap_sem,
-    in_sem, sq_sem, st_sem, pre_sem, back_sem, pipe_s, pipe_r, xg_s, xg_r, gt_s, gt_r, gf_s, gf_r,
+    in_sem, sq_s, sq_r, st_sem, pre_s, pre_r, back_s, back_r, pipe_s, pipe_r, xg_s, xg_r, gt_s, gt_r, gf_s, gf_r,
     r1_s, r1_r, r2_s, r2_r, ri_s, ri_r,
 ):
     steps, vs, tok, wid, rank, nt, npipe, ndp = dims
@@ -163,11 +163,10 @@
     gsr = (gsr0, gsr1)
 
     def x_copies(t, v):
-        base = v * steps + t
         cols = pl.ds(0, GATHERED[v] * cc)
         return to_dp(
             lambda part: x_hbm.at[t, v, :, cols], lambda k: xr[v].at[k, t],
-            lambda k: xg_s.at[base, k], lambda k: xg_r.at[base, k], gather_kind[v],
+            lambda k: xg_s.at[v], lambda k: xg_r.at[v], gather_kind[v],
         )
 
 
@@ -213,7 +212,7 @@
     def sq_copies(v, g):
         base = 2 * v + g
         return to_tensor(
-            sqs.at[v, g], lambda k: sqr.at[k, v, g], lambda k: sq_sem.at[0, base, k], lambda k: sq_sem.at[1, base, k]
+            sqs.at[v, g], lambda k: sqr.at[k, v, g], lambda k: sq_s, lambda k: sq_r.at[base, k]
         )
 
     def prep(v, g):
@@ -243,24 +242,24 @@
 
     def gs_copies(t, v):
         cols = pl.ds(t * tok, tok)
-        base = v * steps + t
         mine = share_of(v)
         source = (lambda part: gs_t.at[v, part, mine, :, cols]) if v == 0 else (lambda part: gs_t.at[v, mine, part, :, cols])
         return to_dp(
             source, lambda k: gsr[v].at[k, mine, :, cols],
-            lambda k: gt_s.at[base, k], lambda k: gt_r.at[base, k], gather_kind[v],
+            lambda k: gt_s.at[v], lambda k: gt_r.at[v], gather_kind[v],
         )
 
-    def pass_copies(t, v):
+    def pass_copies(v):
         if count_of[split_kind[v]] % nt:
             return []
-        cols = pl.ds(t * tok, tok)
-        base = v * steps + t
         out = []
         for k in range(count_of[gather_kind[v]] - 1):
-            piece = gsr[v].at[k, share_of(v), :, cols]
-            out += to_tensor(piece, lambda i: piece, lambda i: gf_s.at[base, k, i], lambda i: gf_r.at[base, k, i])
+            piece = gsr[v].at[k, share_of(v)]
+            out += to_tensor(piece, lambda i: piece, lambda i: gf_s.at[v, k, i], lambda i: gf_r.at[v, k, i])
         return out
+
+    def take_bytes(ref, sem):
+        pltpu.make_async_copy(ref, ref, sem).wait()
 
     pre_copies = {}
     back_copies = {}
@@ -277,7 +276,7 @@
         lax.fori_loop(0, rank // rtile, body, 0)
         base = 2 * v + g
         pre_copies[v, g] = to_tensor(
-            ps.at[v, rows], lambda k: pr.at[k, v, rows], lambda k: pre_sem.at[0, base, k], lambda k: pre_sem.at[1, base, k]
+            ps.at[v, rows], lambda k: pr.at[k, v, rows], lambda k: pre_s, lambda k: pre_r.at[base, k]
         )
         for item in pre_copies[v, g]:
             item.start()
@@ -302,10 +301,10 @@
             return carry
 
         lax.fori_loop(0, rank // rtile, body, 0)
-        base = (v * steps + t) * PARTS + (h or 0)
+        base = v * (1 + (steps - 1) * PARTS) + (0 if h is None else 1 + (t - 1) * PARTS + h)
         back_copies[t, v, h] = to_tensor(
             bs.at[v, t, rows], lambda k: br.at[k, v, t, rows],
-            lambda k: back_sem.at[0, base, k], lambda k: back_sem.at[1, base, k],
+            lambda k: back_s, lambda k: back_r.at[base, k],
         )
         for item in back_copies[t, v, h]:
             item.start()
@@ -357,7 +356,8 @@
         if t < steps - 1 and len(pieces(steps, t, h)) > 1:
             for c in pieces(steps, t, h):
                 part(cols_of(c))
-                send_on(t, v, h, c)
+                if send:
+                    send_on(t, v, h, c)
         else:
             lax.fori_loop(0, wid // tile, body, 0)
             if t < steps - 1 and send:
@@ -377,7 +377,7 @@
         where = (rows_of(h),) if c is None else (rows_of(h), cols_of(c))
         return pltpu.make_async_remote_copy(
             src_ref=ob.at[(t, v) + where], dst_ref=ca.at[(slot, t + 1) + where],
-            send_sem=pipe_s.at[slots[t, v, h, c]], recv_sem=pipe_r.at[slots[t, slot, h, c]],
+            send_sem=pipe_s, recv_sem=pipe_r.at[slots[t, slot, h, c]],
             device_id={"pipe": prev_p}, device_id_type=MESH,
         )
 
@@ -389,20 +389,9 @@
         if v == 1:
             @pl.when(me_p == 0)
             def _():
-                if t == 0 and h == 0:
+                if t == 0 and h == 0 and c == pieces(steps, t, h)[0]:
                     pl.semaphore_wait(wrap_sem, 1)
                 pipe_copy(t, 1, 0, h, c).start()
-
-    def sent_on(t, v, h):
-        for c in pieces(steps, t, h):
-            @pl.when(me_p > 0)
-            def _():
-                pipe_copy(t, v, v, h, c).wait_send()
-
-            if v == 1:
-                @pl.when(me_p == 0)
-                def _():
-                    pipe_copy(t, 1, 0, h, c).wait_send()
 
     def take(t, v, h, only=None):
         want = pieces(steps, t - 1, h)
@@ -456,13 +445,13 @@
         count = count_of[second]
         source = (lambda part: gb.at[e, :, part]) if first == "l" else (lambda part: gb.at[e, part])
         return to_dp(
-            source, lambda k: r1.at[e, k, pl.ds(0, count)], lambda k: r1_s.at[e, k], lambda k: r1_r.at[e, k], first
+            source, lambda k: r1.at[e, k, pl.ds(0, count)], lambda k: r1_s, lambda k: r1_r.at[e, k], first
         )
 
     def join_copies(job):
         e = jobs[job]
         return to_dp(
-            lambda part: p2.at[e, part], lambda k: r2.at[e, k], lambda k: r2_s.at[e, k], lambda k: r2_r.at[e, k],
+            lambda part: p2.at[e, part], lambda k: r2.at[e, k], lambda k: r2_s, lambda k: r2_r.at[e, k],
             axes_of(job)[1],
         )
 
@@ -514,18 +503,16 @@
         base = v * CHUNKS + j
         return to_dp(
             lambda part: p2i.at[v, j, part], lambda k: r2i.at[v, j, k],
-            lambda k: ri_s.at[base, k], lambda k: ri_r.at[base, k], split_kind[v],
+            lambda k: ri_s.at[v], lambda k: ri_r.at[base, k], split_kind[v],
         )
 
     def wait_gathered(v):
-        for t in range(steps):
-            for item in gs_copies(t, v):
-                item.wait_recv()
-            for item in pass_copies(t, v):
-                item.start()
-        for t in range(steps):
-            for item in x_copies(t, v) + pass_copies(t, v):
-                item.wait_recv()
+        take_bytes(gsr[v].at[:, share_of(v)], gt_r.at[v])
+        for item in pass_copies(v):
+            item.start()
+        take_bytes(xr[v], xg_r.at[v])
+        for item in pass_copies(v):
+            item.wait_recv()
 
     def grad_in(v, which):
         width = count_of[split_kind[v]]
@@ -635,23 +622,27 @@
             step(t, 1, h)
         if t == 1:
             for h in halves:
-                send_on(0, 0, h, None)
+                for c in pieces(steps, 0, h):
+                    send_on(0, 0, h, c)
         finish_gs(t, 1)
     for h in halves[:-1]:
         step(last, 1, h)
-    products(1, ORDER[1][:2])
-    for j in ORDER[1][2:]:
-        take(last, 1, PARTS - 1, j)
-    back(last, 1, PARTS - 1)
-    with scope("gout1"):
-        finish_gs(last, 1)
-        for j in ORDER[1][2:]:
-            product(("out", 1, j))
-        for j in rest("in", 1):
-            product(("in", 1, j))
+    def end_products(v):
+        products(v, ORDER[:3])
+        for j in ORDER[3:]:
+            take(last, v, PARTS - 1, j)
+        back(last, v, PARTS - 1)
+        with scope(f"gout{v}"):
+            finish_gs(last, v)
+            for j in ORDER[3:]:
+                product(("out", v, j))
+            for j in rest("in", v):
+                product(("in", v, j))
+
+    end_products(1)
 
     def first_middles():
-        middle(("out", 1, 0))
+        middle(("out", 1, 2))
 
     for t in range(1, last):
         for h in halves:
@@ -661,43 +652,33 @@
                 with scope("wgat1"):
                     wait_gathered(1)
                 with scope("gin1"):
-                    grad_in(1, rest("out", 1)[:1])
+                    grad_in(1, rest("out", 1))
+                    middle(("out", 1, 3))
         finish_gs(t, 0)
-    with scope("mid11"):
+    with scope("mid1"):
+        middle(("out", 1, 0))
         middle(("out", 1, 1))
-        middle(("out", 1, 3))
     for h in halves[:-1]:
         step(last, 0, h)
-    with scope("mid12"):
-        middle(("out", 1, 2))
-    products(0, ORDER[0][:2])
-    for j in ORDER[0][2:]:
-        take(last, 0, PARTS - 1, j)
-    back(last, 0, PARTS - 1)
-    with scope("gout0"):
-        finish_gs(last, 0)
-        for j in ORDER[0][2:]:
-            product(("out", 0, j))
-        for j in rest("in", 0):
-            product(("in", 0, j))
-    with scope("gin1b"):
-        grad_in(1, rest("out", 1)[1:])
+    end_products(0)
     with scope("midi1"):
         for j in rest("in", 1):
             middle(("in", 1, j))
-    with scope("mid0_0"):
-        middle(("out", 0, 0))
     with scope("wgat0"):
         wait_gathered(0)
     with scope("gin0"):
         grad_in(0, rest("out", 0))
+    with scope("final1a"):
+        for j in (2, 3, 0, 1):
+            final(("out", 1, j))
+        for j in rest("out", 1):
+            final_in(1, j)
     with scope("mid0_3"):
         middle(("out", 0, 3))
-    with scope("final1a"):
-        for j in (0, 1, 3):
-            final(("out", 1, j))
-        for j in rest("out", 1)[:1]:
-            final_in(1, j)
+    with scope("mid0_0"):
+        middle(("out", 0, 0))
+    with scope("mid0_2"):
+        middle(("out", 0, 2))
 
     @pl.when(me_p < npipe - 1)
     def _():
@@ -705,24 +686,28 @@
             item.wait_recv()
 
     with scope("drain"):
-        for item in stat_copies("l") + stat_copies("h") + sum([sq_copies(v, g) for v in range(vs) for g in range(2)], []):
+        for item in stat_copies("l") + stat_copies("h"):
             item.wait_send()
-        for items in back_copies.values():
-            for item in items:
+        take_bytes(sqr, sq_s)
+        take_bytes(pr, pre_s)
+        take_bytes(br, back_s)
+
+        @pl.when(me_p > 0)
+        def _():
+            take_bytes(ob, pipe_s)
+
+        @pl.when(me_p == 0)
+        def _():
+            take_bytes(ob.at[:, 1], pipe_s)
+
+        for v in range(vs):
+            take_bytes(xr[v], xg_s.at[v])
+            take_bytes(gsr[v].at[:, share_of(v)], gt_s.at[v])
+            for item in pass_copies(v):
                 item.wait_send()
-        for v in range(vs):
-            for g in range(2):
-                for item in pre_copies[v, g]:
-                    item.wait_send()
-            for t in range(steps):
-                for item in x_copies(t, v) + gs_copies(t, v) + pass_copies(t, v):
-                    item.wait_send()
-                if t < steps - 1:
-                    for h in halves:
-                        sent_on(t, v, h)
-    for j in (1, 2):
-        with scope(f"mid0_{j}"):
-            middle(("out", 0, j))
+
+    with scope("mid0_1"):
+        middle(("out", 0, 1))
     with scope("midi0"):
         for j in rest("in", 0):
             middle(("in", 0, j))
@@ -730,28 +715,28 @@
         for j in rest("out", 0):
             final_in(0, j)
     with scope("final1b"):
-        for j in rest("out", 1)[1:]:
-            final_in(1, j)
         for j in rest("in", 1):
             final(("in", 1, j))
-        final(("out", 1, 2))
     for v in range(vs):
-        for j in range(GATHERED[v]):
-            for item in in_copies(v, j):
-                item.wait_send()
-    for job in jobs:
-        for item in split_copies(job):
-            item.wait_send()
-    for j in (0, 1, 3, 2):
+        take_bytes(r2i.at[v, pl.ds(0, GATHERED[v]), pl.ds(0, count_of[split_kind[v]] - 1)], ri_s.at[v])
+
+    def drain_split(copies, whole, sem):
+        if na == nb:
+            take_bytes(whole, sem)
+        else:
+            for job in jobs:
+                for item in copies(job):
+                    item.wait_send()
+
+    drain_split(split_copies, r1, r1_s)
+    for j in (3, 0, 1, 2):
         with scope(f"fin0_{j}"):
             final(("out", 0, j))
     with scope("fini0"):
         for j in rest("in", 0):
             final(("in", 0, j))
     with scope("tail"):
-        for job in jobs:
-            for item in join_copies(job):
-                item.wait_send()
+        drain_split(join_copies, r2, r2_s)
 
 
 def store(a, b, c, a_out, b_out, c_out, sem):
@@ -826,23 +811,26 @@
         V((hm, 8, lanes), F32),
         pltpu.SemaphoreType.REGULAR,
         DMA((13,)),
-        DMA((2, 2 * vs, peers)),
+        DMA,
+        DMA((2 * vs, peers)),
         DMA((4, less)),
-        DMA((2, 2 * vs, peers)),
-        DMA((2, vs * steps * PARTS, peers)),
+        DMA,
+        DMA((2 * vs, peers)),
+        DMA,
+        DMA((vs * (1 + (steps - 1) * PARTS), peers)),
+        DMA,
         DMA((pipe_count,)),
-        DMA((pipe_count,)),
-        DMA((vs * steps, less)),
-        DMA((vs * steps, less)),
-        DMA((vs * steps, less)),
-        DMA((vs * steps, less)),
-        DMA((vs * steps, less, peers)),
-        DMA((vs * steps, less, peers)),
+        DMA((vs,)),
+        DMA((vs,)),
+        DMA((vs,)),
+        DMA((vs,)),
+        DMA((vs, less, peers)),
+        DMA((vs, less, peers)),
+        DMA,
         DMA((jobs, less)),
+        DMA,
         DMA((jobs, less)),
-        DMA((jobs, less)),
-        DMA((jobs, less)),
-        DMA((vs * CHUNKS, less)),
+        DMA((vs,)),
         DMA((vs * CHUNKS, less)),
     ]
     grad_in, grad_out, leaving = pl.pallas_call(

time: 91.7 us -> 90.1 us (0.983)
  Pallas kernels: 90.7 us -> 89.1 us
    pallas_call x1, Pallas kernels: 88.4 us -> 86.7 us  [shards(): pl.pallas_call(functools.partial(kernel, dims), out_shape=(V((vs, rc, wid...]
where the time goes in v4:
time: 90.1 us; the launch traced here: 89.9 us
  Pallas kernels  89.1 us (99%)
    pallas_call x1, Pallas kernels, shards(): pl.pallas_call(functools.partial(kernel, dims), out_shape=(V((vs, rc, wid...  86.7 us
    pallas_call x1, Pallas kernels, shards(): pl.pallas_call(store, out_shape=tuple((jax.ShapeDtypeStruct(a.shape, a.dt...  2.38 us

profile of v4, /device:TPU:0, one launch (start us, length us, event | category | flops | bytes accessed | tf_op | source)
XLA Modules:
  0.0 89.9 jit_solution(15515268652481179155)
XLA Ops:
  0.6 86.7 %shard_map.112 = (f32[2,128,2048]{2,1,0:T(8,128)S(1)}, f32[2,128,2048]{2,1,0:T(8,128)S(1)}, bf16[2,128,2048]{2,1,0:T(8,128)(2,1)S(1)}) custom-call(bf16[3,2,128,2048]{3,2,1,0:T(8,128)(2,1)} %bitcast.15, bf16[2,512,2048]{2,1,0:T(8,128)(2,1)} %bitcast.13, bf16[2,512,2048]{2,1,0:T(8,128)(2,1)} %bitcast.14, f32[2,1,2048]{2,1,0:T(1,128)} %gn_hbm.1, ...), custom_call_target="tpu_custom_call" | custom-call | tf_op jit(solution)/shard_map/pallas_call | solution.py:836
  87.4 2.4 %shard_map.113 = (f32[2,128,2048]{2,1,0:T(8,128)}, f32[2,128,2048]{2,1,0:T(8,128)}, bf16[2,128,2048]{2,1,0:T(8,128)(2,1)}) custom-call(f32[2,128,2048]{2,1,0:T(8,128)S(1)} %get-tuple-element.9.a, f32[2,128,2048]{2,1,0:T(8,128)S(1)} %get-tuple-element.10.b, bf16[2,128,2048]{2,1,0:T(8,128)(2,1)S(1)} %get-tuple-element.11.c), custom_call_target="tpu_custom_call" | custom-call | tf_op jit(solution)/shard_map/pallas_call | solution.py:853

commit v5 on v4

--- a/solution.py
+++ b/solution.py
@@ -499,11 +499,13 @@
         dest = fo if what == "out" else fi
         dest[v, :, cols_of(j)] = total * scale
 
+    def in_bytes(v):
+        return r2i.at[v, pl.ds(0, GATHERED[v]), pl.ds(0, count_of[split_kind[v]] - 1)]
+
     def in_copies(v, j):
-        base = v * CHUNKS + j
         return to_dp(
             lambda part: p2i.at[v, j, part], lambda k: r2i.at[v, j, k],
-            lambda k: ri_s.at[v], lambda k: ri_r.at[base, k], split_kind[v],
+            lambda k: ri_s.at[v], lambda k: ri_r.at[v], split_kind[v],
         )
 
     def wait_gathered(v):
@@ -532,14 +534,14 @@
             for item in in_copies(v, j):
                 item.start()
 
-    def final_in(v, j):
-        for item in in_copies(v, j):
-            item.wait_recv()
+    def final_in(v):
+        take_bytes(in_bytes(v), ri_r.at[v])
         along_h = split_kind[v] == "h"
-        total = p2i[v, j, me_h if along_h else me_l].astype(F32)
-        for k in range(count_of[split_kind[v]] - 1):
-            total = total + r2i[v, j, k].astype(F32)
-        fi[v, :, cols_of(j)] = total * scale
+        for j in range(GATHERED[v]):
+            total = p2i[v, j, me_h if along_h else me_l].astype(F32)
+            for k in range(count_of[split_kind[v]] - 1):
+                total = total + r2i[v, j, k].astype(F32)
+            fi[v, :, cols_of(j)] = total * scale
 
     last = steps - 1
 
@@ -664,6 +666,10 @@
     with scope("midi1"):
         for j in rest("in", 1):
             middle(("in", 1, j))
+    with scope("mid0_3"):
+        middle(("out", 0, 3))
+    with scope("mid0_0"):
+        middle(("out", 0, 0))
     with scope("wgat0"):
         wait_gathered(0)
     with scope("gin0"):
@@ -671,12 +677,7 @@
     with scope("final1a"):
         for j in (2, 3, 0, 1):
             final(("out", 1, j))
-        for j in rest("out", 1):
-            final_in(1, j)
-    with scope("mid0_3"):
-        middle(("out", 0, 3))
-    with scope("mid0_0"):
-        middle(("out", 0, 0))
+        final_in(1)
     with scope("mid0_2"):
         middle(("out", 0, 2))
 
@@ -712,13 +713,12 @@
         for j in rest("in", 0):
             middle(("in", 0, j))
     with scope("final0i"):
-        for j in rest("out", 0):
-            final_in(0, j)
+        final_in(0)
     with scope("final1b"):
         for j in rest("in", 1):
             final(("in", 1, j))
     for v in range(vs):
-        take_bytes(r2i.at[v, pl.ds(0, GATHERED[v]), pl.ds(0, count_of[split_kind[v]] - 1)], ri_s.at[v])
+        take_bytes(in_bytes(v), ri_s.at[v])
 
     def drain_split(copies, whole, sem):
         if na == nb:
@@ -740,11 +740,15 @@
 
 
 def store(a, b, c, a_out, b_out, c_out, sem):
-    copies = [pltpu.make_async_copy(*pair, sem.at[k]) for k, pair in enumerate(((a, a_out), (b, b_out), (c, c_out)))]
-    for item in copies:
-        item.start()
-    for item in copies:
-        item.wait()
+    pairs = ((a, a_out), (b, b_out), (c, c_out))
+    for k, (src, dst) in enumerate(pairs):
+        rows = src.shape[1] // 2
+        for v in range(src.shape[0]):
+            for r in range(2):
+                where = (v, pl.ds(r * rows, rows))
+                pltpu.make_async_copy(src.at[where], dst.at[where], sem.at[k]).start()
+    for k, pair in enumerate(pairs):
+        pltpu.make_async_copy(*pair, sem.at[k]).wait()
 
 
 def shards(
@@ -831,7 +835,7 @@
         DMA,
         DMA((jobs, less)),
         DMA((vs,)),
-        DMA((vs * CHUNKS, less)),
+        DMA((vs,)),
     ]
     grad_in, grad_out, leaving = pl.pallas_call(
         functools.partial(kernel, dims),

time: 90.1 us -> 88.7 us (0.984)
  Pallas kernels: 89.1 us -> 87.7 us
    pallas_call x1, Pallas kernels: 86.7 us -> 85.4 us  [shards(): pl.pallas_call(functools.partial(kernel, dims), out_shape=(V((vs, rc, wid...]
where the time goes in v5:
time: 88.7 us; the launch traced here: 88.5 us
  Pallas kernels  87.7 us (99%)
    pallas_call x1, Pallas kernels, shards(): pl.pallas_call(functools.partial(kernel, dims), out_shape=(V((vs, rc, wid...  85.4 us
    pallas_call x1, Pallas kernels, shards(): pl.pallas_call(store, out_shape=tuple((jax.ShapeDtypeStruct(a.shape, a.dt...  2.35 us

profile of v5, /device:TPU:0, one launch (start us, length us, event | category | flops | bytes accessed | tf_op | source)
XLA Modules:
  0.0 88.5 jit_solution(14074621429460486322)
XLA Ops:
  0.6 85.4 %shard_map.112 = (f32[2,128,2048]{2,1,0:T(8,128)S(1)}, f32[2,128,2048]{2,1,0:T(8,128)S(1)}, bf16[2,128,2048]{2,1,0:T(8,128)(2,1)S(1)}) custom-call(bf16[3,2,128,2048]{3,2,1,0:T(8,128)(2,1)} %bitcast.15, bf16[2,512,2048]{2,1,0:T(8,128)(2,1)} %bitcast.13, bf16[2,512,2048]{2,1,0:T(8,128)(2,1)} %bitcast.14, f32[2,1,2048]{2,1,0:T(1,128)} %gn_hbm.1, ...), custom_call_target="tpu_custom_call" | custom-call | tf_op jit(solution)/shard_map/pallas_call | solution.py:840
  86.0 2.3 %shard_map.113 = (f32[2,128,2048]{2,1,0:T(8,128)}, f32[2,128,2048]{2,1,0:T(8,128)}, bf16[2,128,2048]{2,1,0:T(8,128)(2,1)}) custom-call(f32[2,128,2048]{2,1,0:T(8,128)S(1)} %get-tuple-element.9.a, f32[2,128,2048]{2,1,0:T(8,128)S(1)} %get-tuple-element.10.b, bf16[2,128,2048]{2,1,0:T(8,128)(2,1)S(1)} %get-tuple-element.11.c), custom_call_target="tpu_custom_call" | custom-call | tf_op jit(solution)/shard_map/pallas_call | solution.py:857

commit v6 on v5

--- a/solution.py
+++ b/solution.py
@@ -27,6 +27,7 @@
 
 CHUNKS = 4
 GATHERED = (3, 3)
+EXTRA = -128
 PARTS = 2
 FIRST_AXIS = ("hhll", "hllh")
 IN_AXIS = ("h", "l")
@@ -163,7 +164,7 @@
     gsr = (gsr0, gsr1)
 
     def x_copies(t, v):
-        cols = pl.ds(0, GATHERED[v] * cc)
+        cols = pl.ds(0, GATHERED[v] * cc - EXTRA)
         return to_dp(
             lambda part: x_hbm.at[t, v, :, cols], lambda k: xr[v].at[k, t],
             lambda k: xg_s.at[v], lambda k: xg_r.at[v], gather_kind[v],
@@ -439,20 +440,31 @@
         first = FIRST_AXIS[v][j] if what == "out" else IN_AXIS[v]
         return ("l", "h") if first == "l" else ("h", "l")
 
+    def width_of(job):
+        return cc if job[0] == "out" else cc + EXTRA
+
+    def span_of(job):
+        return cols_of(job[2]) if job[0] == "out" else pl.ds(wid - cc - EXTRA, cc + EXTRA)
+
     def split_copies(job):
         e = jobs[job]
         first, second = axes_of(job)
         count = count_of[second]
-        source = (lambda part: gb.at[e, :, part]) if first == "l" else (lambda part: gb.at[e, part])
+        lanes_of = pl.ds(0, width_of(job))
+        kind = 0 if job[0] == "out" else 1
+        source = (lambda part: gb.at[e, :, part, :, lanes_of]) if first == "l" else (lambda part: gb.at[e, part, :, :, lanes_of])
         return to_dp(
-            source, lambda k: r1.at[e, k, pl.ds(0, count)], lambda k: r1_s, lambda k: r1_r.at[e, k], first
+            source, lambda k: r1.at[e, k, pl.ds(0, count), :, lanes_of],
+            lambda k: r1_s.at[kind], lambda k: r1_r.at[e, k], first,
         )
 
     def join_copies(job):
         e = jobs[job]
+        lanes_of = pl.ds(0, width_of(job))
+        kind = 0 if job[0] == "out" else 1
         return to_dp(
-            lambda part: p2.at[e, part], lambda k: r2.at[e, k], lambda k: r2_s, lambda k: r2_r.at[e, k],
-            axes_of(job)[1],
+            lambda part: p2.at[e, part, :, lanes_of], lambda k: r2.at[e, k, :, lanes_of],
+            lambda k: r2_s.at[kind], lambda k: r2_r.at[e, k], axes_of(job)[1],
         )
 
     def product(job):
@@ -464,10 +476,10 @@
             )
         else:
             value = jnp.dot(
-                gs_t[v].reshape(rank, steps * tok), xs[:, v, :, cols_of(j)].reshape(steps * tok, cc),
+                gs_t[v].reshape(rank, steps * tok), xs[:, v, :, span_of(job)].reshape(steps * tok, width_of(job)),
                 preferred_element_type=F32,
-            ) * gn_ref[v, :, cols_of(j)]
-        gb[e] = value.astype(BF16).reshape(na, nb, rc, cc)
+            ) * gn_ref[v, :, span_of(job)]
+        gb[e, :, :, :, :width_of(job)] = value.astype(BF16).reshape(na, nb, rc, width_of(job))
         for item in split_copies(job):
             item.start()
 
@@ -477,11 +489,12 @@
         count = count_of[second]
         for item in split_copies(job):
             item.wait_recv()
-        own = gb[e, :, me_l] if first == "l" else gb[e, me_h]
+        w = width_of(job)
+        own = gb[e, :, me_l, :, :w] if first == "l" else gb[e, me_h, :, :, :w]
         total = own.astype(F32)
         for k in range(count_of[first] - 1):
-            total = total + r1[e, k, :count].astype(F32)
-        p2[e, :count] = total.astype(BF16)
+            total = total + r1[e, k, :count, :, :w].astype(F32)
+        p2[e, :count, :, :w] = total.astype(BF16)
         for item in join_copies(job):
             item.start()
 
@@ -493,18 +506,23 @@
         kind = axes_of(job)[1]
         for item in join_copies(job):
             item.wait_recv()
-        total = p2[e, me_h if kind == "h" else me_l].astype(F32)
+        w = width_of(job)
+        total = p2[e, me_h if kind == "h" else me_l, :, :w].astype(F32)
         for k in range(count_of[kind] - 1):
-            total = total + r2[e, k].astype(F32)
+            total = total + r2[e, k, :, :w].astype(F32)
         dest = fo if what == "out" else fi
-        dest[v, :, cols_of(j)] = total * scale
+        dest[v, :, span_of(job)] = total * scale
 
     def in_bytes(v):
-        return r2i.at[v, pl.ds(0, GATHERED[v]), pl.ds(0, count_of[split_kind[v]] - 1)]
+        return r2i.at[v, pl.ds(0, count_of[split_kind[v]] - 1)]
+
+    def in_cols(v, j):
+        return pl.ds(j * cc, cc - EXTRA if j == GATHERED[v] - 1 else cc)
 
     def in_copies(v, j):
+        cols = in_cols(v, j)
         return to_dp(
-            lambda part: p2i.at[v, j, part], lambda k: r2i.at[v, j, k],
+            lambda part: p2i.at[v, part, :, cols], lambda k: r2i.at[v, k, :, cols],
             lambda k: ri_s.at[v], lambda k: ri_r.at[v], split_kind[v],
         )
 
@@ -521,16 +539,16 @@
         own = gs_t[v, me_h] if v == 0 else gs_t[v, :, me_l]
         own = own.reshape(width * rc, steps * tok)
         for j in which:
-            value = jnp.dot(
-                own, xs[:, v, :, cols_of(j)].reshape(steps * tok, cc), preferred_element_type=F32
-            )
+            cols = in_cols(v, j)
+            w = cols.size
+            value = jnp.dot(own, xs[:, v, :, cols].reshape(steps * tok, w), preferred_element_type=F32)
             for k in range(count_of[gather_kind[v]] - 1):
                 left = gsr[v][k].reshape(width * rc, steps * tok)
                 value = value + jnp.dot(
-                    left, xr[v][k, :, :, cols_of(j)].reshape(steps * tok, cc), preferred_element_type=F32
+                    left, xr[v][k, :, :, cols].reshape(steps * tok, w), preferred_element_type=F32
                 )
-            value = value * gn_ref[v, :, cols_of(j)]
-            p2i[v, j, :width] = value.astype(BF16).reshape(width, rc, cc)
+            value = value * gn_ref[v, :, cols]
+            p2i[v, :width, :, cols] = value.astype(BF16).reshape(width, rc, w)
             for item in in_copies(v, j):
                 item.start()
 
@@ -538,10 +556,11 @@
         take_bytes(in_bytes(v), ri_r.at[v])
         along_h = split_kind[v] == "h"
         for j in range(GATHERED[v]):
-            total = p2i[v, j, me_h if along_h else me_l].astype(F32)
+            cols = in_cols(v, j)
+            total = p2i[v, me_h if along_h else me_l, :, cols].astype(F32)
             for k in range(count_of[split_kind[v]] - 1):
-                total = total + r2i[v, j, k].astype(F32)
-            fi[v, :, cols_of(j)] = total * scale
+                total = total + r2i[v, k, :, cols].astype(F32)
+            fi[v, :, cols] = total * scale
 
     last = steps - 1
 
@@ -630,13 +649,14 @@
     for h in halves[:-1]:
         step(last, 1, h)
     def end_products(v):
-        products(v, ORDER[:3])
-        for j in ORDER[3:]:
+        ahead = 2 + v
+        products(v, ORDER[:ahead])
+        for j in ORDER[ahead:]:
             take(last, v, PARTS - 1, j)
         back(last, v, PARTS - 1)
         with scope(f"gout{v}"):
             finish_gs(last, v)
-            for j in ORDER[3:]:
+            for j in ORDER[ahead:]:
                 product(("out", v, j))
             for j in rest("in", v):
                 product(("in", v, j))
@@ -668,8 +688,6 @@
             middle(("in", 1, j))
     with scope("mid0_3"):
         middle(("out", 0, 3))
-    with scope("mid0_0"):
-        middle(("out", 0, 0))
     with scope("wgat0"):
         wait_gathered(0)
     with scope("gin0"):
@@ -678,6 +696,8 @@
         for j in (2, 3, 0, 1):
             final(("out", 1, j))
         final_in(1)
+    with scope("mid0_0"):
+        middle(("out", 0, 0))
     with scope("mid0_2"):
         middle(("out", 0, 2))
 
@@ -720,9 +740,13 @@
     for v in range(vs):
         take_bytes(in_bytes(v), ri_s.at[v])
 
-    def drain_split(copies, whole, sem):
+    outs = vs * CHUNKS
+
+    def drain_split(copies, landed, sem):
         if na == nb:
-            take_bytes(whole, sem)
+            rows = (slice(None),) * (len(landed.shape) - 2)
+            take_bytes(landed.at[(pl.ds(0, outs),) + rows + (pl.ds(0, cc),)], sem.at[0])
+            take_bytes(landed.at[(pl.ds(outs, len(jobs) - outs),) + rows + (pl.ds(0, cc + EXTRA),)], sem.at[1])
         else:
             for job in jobs:
                 for item in copies(job):
@@ -792,8 +816,8 @@
         V((vs, na, nb, rc, steps * tok), BF16),
         V((hm, nb, rc, steps * tok), BF16),
         V((lm, na, rc, steps * tok), BF16),
-        V((hm, steps, tok, GATHERED[0] * cc), BF16),
-        V((lm, steps, tok, GATHERED[1] * cc), BF16),
+        V((hm, steps, tok, GATHERED[0] * cc - EXTRA), BF16),
+        V((lm, steps, tok, GATHERED[1] * cc - EXTRA), BF16),
         V((vs, steps, tok, rank), BF16),
         V((peers, vs, steps, tok, rank), BF16),
         V((steps - 1, vs, tok, wid), BF16),
@@ -802,12 +826,12 @@
         V((vs, 2, tok, 128), F32),
         V((2, 8, lanes), F32),
         V((lm, 8, lanes), F32),
-        V((jobs, na, nb, rc, cc), BF16),
-        V((jobs, less, pmax, rc, cc), BF16),
-        V((jobs, pmax, rc, cc), BF16),
-        V((jobs, less, rc, cc), BF16),
-        V((vs, CHUNKS, pmax, rc, cc), BF16),
-        V((vs, CHUNKS, less, rc, cc), BF16),
+        V((jobs, na, nb, rc, cc + max(EXTRA, 0)), BF16),
+        V((jobs, less, pmax, rc, cc + max(EXTRA, 0)), BF16),
+        V((jobs, pmax, rc, cc + max(EXTRA, 0)), BF16),
+        V((jobs, less, rc, cc + max(EXTRA, 0)), BF16),
+        V((vs, pmax, rc, wid - cc - EXTRA), BF16),
+        V((vs, less, rc, wid - cc - EXTRA), BF16),
         V(norm_gain.shape, F32),
         pltpu.SMEM(rewards.shape, F32),
         pltpu.SMEM(seq_lengths.shape, jnp.int32),
@@ -830,9 +854,9 @@
         DMA((vs,)),
         DMA((vs, less, peers)),
         DMA((vs, less, peers)),
-        DMA,
+        DMA((2,)),
         DMA((jobs, less)),
-        DMA,
+        DMA((2,)),
         DMA((jobs, less)),
         DMA((vs,)),
         DMA((vs,)),

time: 88.7 us -> 88.2 us (level)
  no operation moved by 1% of the time
where the time goes in v6:
time: 88.2 us; the launch traced here: 88 us
  Pallas kernels  87.2 us (99%)
    pallas_call x1, Pallas kernels, shards(): pl.pallas_call(functools.partial(kernel, dims), out_shape=(V((vs, rc, wid...  84.9 us
    pallas_call x1, Pallas kernels, shards(): pl.pallas_call(store, out_shape=tuple((jax.ShapeDtypeStruct(a.shape, a.dt...  2.35 us

profile of v6, /device:TPU:0, one launch (start us, length us, event | category | flops | bytes accessed | tf_op | source)
XLA Modules:
  0.0 88.0 jit_solution(16953309877101083413)
XLA Ops:
  0.6 84.9 %shard_map.112 = (f32[2,128,2048]{2,1,0:T(8,128)S(1)}, f32[2,128,2048]{2,1,0:T(8,128)S(1)}, bf16[2,128,2048]{2,1,0:T(8,128)(2,1)S(1)}) custom-call(bf16[3,2,128,2048]{3,2,1,0:T(8,128)(2,1)} %bitcast.15, bf16[2,512,2048]{2,1,0:T(8,128)(2,1)} %bitcast.13, bf16[2,512,2048]{2,1,0:T(8,128)(2,1)} %bitcast.14, f32[2,1,2048]{2,1,0:T(1,128)} %gn_hbm.1, ...), custom_call_target="tpu_custom_call" | custom-call | tf_op jit(solution)/shard_map/pallas_call | solution.py:864
  85.5 2.3 %shard_map.113 = (f32[2,128,2048]{2,1,0:T(8,128)}, f32[2,128,2048]{2,1,0:T(8,128)}, bf16[2,128,2048]{2,1,0:T(8,128)(2,1)}) custom-call(f32[2,128,2048]{2,1,0:T(8,128)S(1)} %get-tuple-element.9.a, f32[2,128,2048]{2,1,0:T(8,128)S(1)} %get-tuple-element.10.b, bf16[2,128,2048]{2,1,0:T(8,128)(2,1)S(1)} %get-tuple-element.11.c), custom_call_target="tpu_custom_call" | custom-call | tf_op jit(solution)/shard_map/pallas_call | solution.py:881

commit v7 on v6

--- a/solution.py
+++ b/solution.py
@@ -47,7 +47,13 @@
 
 def pipe_slots(steps, vs):
     keys = [(t, v, h, c) for t in range(steps - 1) for v in range(vs) for h in range(PARTS) for c in pieces(steps, t, h)]
-    return {key: k for k, key in enumerate(keys)}
+    names = list(dict.fromkeys(shared_key(steps, key) for key in keys))
+    return {key: names.index(shared_key(steps, key)) for key in keys}
+
+
+def shared_key(steps, key):
+    t, v, h, c = key
+    return key if (t, h) == (steps - 2, PARTS - 1) else (t, v, h, None)
 
 
 def kernel(
@@ -399,15 +405,22 @@
         first = only is None or only == want[0]
         if only is not None:
             want = (only,)
+        together = (t - 1, h) != (steps - 2, PARTS - 1)
+
+        def arrive():
+            if together:
+                take_bytes(ca.at[v, t, rows_of(h)], pipe_r.at[slots[t - 1, v, h, want[0]]])
+            else:
+                for c in want:
+                    pipe_copy(t - 1, v, v, h, c).wait_recv()
+
         if v == 0:
-            for c in want:
-                pipe_copy(t - 1, v, v, h, c).wait_recv()
+            arrive()
             return
 
         @pl.when(me_p < npipe - 1)
         def _():
-            for c in want:
-                pipe_copy(t - 1, v, v, h, c).wait_recv()
+            arrive()
 
         if first:
             @pl.when(me_p == npipe - 1)
@@ -790,7 +803,7 @@
     rc = rank // ndp
     cc = wid // CHUNKS
     jobs = len(reductions())
-    pipe_count = len(pipe_slots(steps, vs))
+    pipe_count = len(set(pipe_slots(steps, vs).values()))
     hm, lm = max(na - 1, 1), max(nb - 1, 1)
     dims = (steps, vs, tok, wid, rank, nt, npipe, ndp)
     peers = max(nt - 1, 1)

time: 88.2 us -> 88.2 us (level)
  no operation moved by 1% of the time
where the time goes in v7:
time: 88.2 us; the launch traced here: 88 us
  Pallas kernels  87.2 us (99%)
    pallas_call x1, Pallas kernels, shards(): pl.pallas_call(functools.partial(kernel, dims), out_shape=(V((vs, rc, wid...  84.8 us
    pallas_call x1, Pallas kernels, shards(): pl.pallas_call(store, out_shape=tuple((jax.ShapeDtypeStruct(a.shape, a.dt...  2.35 us

profile of v7, /device:TPU:0, one launch (start us, length us, event | category | flops | bytes accessed | tf_op | source)
XLA Modules:
  0.0 88.0 jit_solution(11782485386860788546)
XLA Ops:
  0.6 84.8 %shard_map.112 = (f32[2,128,2048]{2,1,0:T(8,128)S(1)}, f32[2,128,2048]{2,1,0:T(8,128)S(1)}, bf16[2,128,2048]{2,1,0:T(8,128)(2,1)S(1)}) custom-call(bf16[3,2,128,2048]{3,2,1,0:T(8,128)(2,1)} %bitcast.15, bf16[2,512,2048]{2,1,0:T(8,128)(2,1)} %bitcast.13, bf16[2,512,2048]{2,1,0:T(8,128)(2,1)} %bitcast.14, f32[2,1,2048]{2,1,0:T(1,128)} %gn_hbm.1, ...), custom_call_target="tpu_custom_call" | custom-call | tf_op jit(solution)/shard_map/pallas_call | solution.py:877
  85.5 2.3 %shard_map.113 = (f32[2,128,2048]{2,1,0:T(8,128)}, f32[2,128,2048]{2,1,0:T(8,128)}, bf16[2,128,2048]{2,1,0:T(8,128)(2,1)}) custom-call(f32[2,128,2048]{2,1,0:T(8,128)S(1)} %get-tuple-element.9.a, f32[2,128,2048]{2,1,0:T(8,128)S(1)} %get-tuple-element.10.b, bf16[2,128,2048]{2,1,0:T(8,128)(2,1)S(1)} %get-tuple-element.11.c), custom_call_target="tpu_custom_call" | custom-call | tf_op jit(solution)/shard_map/pallas_call | solution.py:894
